TPU v7x, 32 devices: a whole 2x2x4 slice. The times are simulated.
32 devices in a mesh: lon: 8 (over z, x), ch: 4 (over y, core).
Axes of the slice: x: 2, y: 2, z: 4, core: 2. Of those that a mesh axis runs over, the one named last changes fastest.
Arguments:
- grid_inputs: bfloat16 [230400, 474], P('lon'), may hold values from -6 to 6
- embed_weight: bfloat16 [474, 512], replicated, may hold values from -0.25 to 0.25
- embed_bias: float32 [512], replicated, may hold values from -3 to 3
- mesh_latent: bfloat16 [5120, 512], P('lon', 'ch'), may hold values from -6 to 6
- edge_features: bfloat16 [4, 180224], P(None, 'lon'), may hold values from -6 to 6
- senders: int32 [180224], P('lon'), may hold values from 0 to 230399, as said below
- receivers: int32 [180224], P('lon'), may hold values from 0 to 5119, as said below
- sender_weight: bfloat16 [512, 512], P(None, 'ch'), may hold values from -0.25 to 0.25
- receiver_weight: bfloat16 [512, 512], P(None, 'ch'), may hold values from -0.25 to 0.25
- feature_weight: bfloat16 [4, 512], P(None, 'ch'), may hold values from -3 to 3
- hidden_bias: float32 [512], P('ch'), may hold values from -3 to 3
- message_weight: bfloat16 [512, 512], P('ch'), may hold values from -0.25 to 0.25
- message_bias: float32 [512], replicated, may hold values from -1.2 to 1.2
- norm_gain: float32 [512], P('ch'), may hold values from 0.5 to 1.5
- norm_shift: float32 [512], P('ch'), may hold values from -3 to 3
Outputs:
- mesh_out: bfloat16 [5120, 512], P('lon', 'ch')
Inputs may be any that keep to these rules, and one draw needn't show every extreme that they name: Edge e belongs to block b = e // 22528. Its sender is c * 640 + t with latitude row t and a column c that lies, counted around the closed circle of 360 columns, at most 4 columns before or after the block's own columns b * 45 to b * 45 + 44; some block reaches 4 columns on both sides. Within each aligned run of min(2048, 22528) edges of a block, the senders' columns, counted from the block's first widened column, lie within 7 consecutive columns. `receivers`: the receiver of edge e lies among the mesh nodes b * 640 to b * 640 + 639 of its block b = e // 22528; a mesh node may receive no edge.
All inputs are finite; a program needn't handle non-finite values.
Results may differ from a plain program's by a relative error of at most 0.0028.
Values may be sent and summed in bfloat16 or wider, within the bound.
A program may use at most 128 MiB of HBM per device.

v0:
```python
import functools

import jax
import jax.numpy as jnp
from jax import lax
from jax.experimental import pallas as pl
from jax.experimental.pallas import tpu as pltpu
from jax.sharding import PartitionSpec as P

LAT = 640
HALO = 4
CHUNK = 256


def silu(v):
    half = 0.5 * v
    return half + half * jnp.tanh(half)


def dense_kernel(
    steps,
    x_ref,
    embed_ref,
    bias_ref,
    sender_ref,
    mesh_ref,
    message_ref,
    out_ref,
    low_ref,
    high_ref,
    mesh_all_ref,
    message_all_ref,
    first_columns,
    last_columns,
    gather_send,
    gather_recv,
    halo_send,
    halo_recv,
    local_sem,
):
    step = pl.program_id(0)
    lon_count, ch_count = lax.axis_size("lon"), lax.axis_size("ch")
    lon_place, ch_place = lax.axis_index("lon"), lax.axis_index("ch")
    right = lax.rem(lon_place + 1, lon_count)
    left = lax.rem(lon_place + lon_count - 1, lon_count)
    halo_rows = low_ref.shape[0]
    pairs = ((mesh_ref, mesh_all_ref), (message_ref, message_all_ref))
    local = [
        pltpu.make_async_copy(ref, all_ref.at[ch_place], local_sem.at[n])
        for n, (ref, all_ref) in enumerate(pairs)
    ]
    partners = [lax.rem(ch_place + j, ch_count) for j in range(1, ch_count)]
    gathers = [
        pltpu.make_async_remote_copy(
            src_ref=ref,
            dst_ref=all_ref.at[ch_place],
            send_sem=gather_send.at[n, j],
            recv_sem=gather_recv.at[n, j],
            device_id={"ch": partner},
            device_id_type=pl.DeviceIdType.MESH,
        )
        for n, (ref, all_ref) in enumerate(pairs)
        for j, partner in enumerate(partners)
    ]
    halos = [
        pltpu.make_async_remote_copy(
            src_ref=src,
            dst_ref=dst,
            send_sem=halo_send.at[n],
            recv_sem=halo_recv.at[n],
            device_id={"lon": side},
            device_id_type=pl.DeviceIdType.MESH,
        )
        for n, (src, dst, side) in enumerate(
            ((first_columns, high_ref, left), (last_columns, low_ref, right))
        )
    ]

    @pl.when(step == 0)
    def _():
        barrier = pltpu.get_barrier_semaphore()
        for partner in partners:
            pl.semaphore_signal(
                barrier, inc=1, device_id={"ch": partner}, device_id_type=pl.DeviceIdType.MESH
            )
        for side in (left, right):
            pl.semaphore_signal(
                barrier, inc=1, device_id={"lon": side}, device_id_type=pl.DeviceIdType.MESH
            )
        pl.semaphore_wait(barrier, ch_count + 1)
        for copy in gathers + local:
            copy.start()

    for n, copy in enumerate(halos):
        pl.when(step == n + 1)(copy.start)

    before = (
        lax.dot_general(
            x_ref[...], embed_ref[...], (((0,), (0,)), ((), ())),
            preferred_element_type=jnp.float32,
        )
        + bias_ref[...]
    )
    latent = silu(before).astype(jnp.bfloat16)
    out_ref[...] = jnp.dot(latent, sender_ref[...], preferred_element_type=jnp.float32)

    @pl.when(step == 0)
    def _():
        first_columns[...] = out_ref[:halo_rows, :].astype(jnp.bfloat16)

    @pl.when(step == 1)
    def _():
        last_columns[...] = out_ref[out_ref.shape[0] - halo_rows:, :].astype(jnp.bfloat16)

    @pl.when(step == steps - 1)
    def _():
        for copy in gathers + halos + local:
            copy.wait()


def sender_terms(
    grid_inputs, embed_weight, embed_bias, sender_weight, mesh_latent, message_weight
):
    channels, full_width = embed_weight.shape
    width = sender_weight.shape[1]
    points = grid_inputs.shape[0]
    columns = points // LAT
    group = max(n for n in range(1, 6) if columns % n == 0)
    steps = columns // group
    assert group >= HALO and steps > 2
    rows = group * LAT
    ch_count = lax.axis_size("ch")

    def place(i):
        return jnp.where(i == 1, steps - 1, jnp.maximum(i - 1, 0))

    whole = lambda shape: pl.BlockSpec(shape, lambda i: (0, 0))
    hbm = pl.BlockSpec(memory_space=pl.ANY)
    halo = (HALO * LAT, width)
    return pl.pallas_call(
        functools.partial(dense_kernel, steps),
        grid=(steps,),
        in_specs=[
            pl.BlockSpec((channels, rows), lambda i: (0, place(i))),
            whole((channels, full_width)),
            whole((1, full_width)),
            whole((full_width, width)),
            hbm,
            hbm,
        ],
        out_specs=[pl.BlockSpec((rows, width), lambda i: (place(i), 0)), hbm, hbm, hbm, hbm],
        out_shape=[
            jax.ShapeDtypeStruct((points, width), jnp.float32),
            jax.ShapeDtypeStruct(halo, jnp.bfloat16),
            jax.ShapeDtypeStruct(halo, jnp.bfloat16),
            jax.ShapeDtypeStruct((ch_count, *mesh_latent.shape), jnp.bfloat16),
            jax.ShapeDtypeStruct((ch_count, *message_weight.shape), jnp.bfloat16),
        ],
        scratch_shapes=[
            pltpu.VMEM(halo, jnp.bfloat16),
            pltpu.VMEM(halo, jnp.bfloat16),
            pltpu.SemaphoreType.DMA((2, ch_count - 1)),
            pltpu.SemaphoreType.DMA((2, ch_count - 1)),
            pltpu.SemaphoreType.DMA((2,)),
            pltpu.SemaphoreType.DMA((2,)),
            pltpu.SemaphoreType.DMA((2,)),
        ],
        compiler_params=pltpu.CompilerParams(
            vmem_limit_bytes=56 << 20, collective_id=0, has_side_effects=True
        ),
        cost_estimate=pl.CostEstimate(
            flops=2 * points * full_width * (channels + width),
            bytes_accessed=points * (2 * channels + 4 * width),
            transcendentals=points * full_width,
        ),
    )(grid_inputs.T, embed_weight, embed_bias.reshape(1, -1), sender_weight,
      mesh_latent, message_weight)


def edge_kernel(
    send_ref,
    recv_ref,
    own_ref,
    low_ref,
    high_ref,
    mesh_all_ref,
    receiver_ref,
    hidden_bias_ref,
    recv_row_ref,
    features_ref,
    feature_weight_ref,
    out_ref,
    tally_ref,
    table,
    recv_terms_ref,
    even,
    odd,
    total,
    sem,
):
    own_rows = own_ref.shape[0]
    halo_rows = low_ref.shape[0]
    copy = pltpu.make_async_copy(own_ref, table.at[pl.ds(halo_rows, own_rows)], sem)
    copy.start()
    table[:halo_rows, :] = low_ref[...].astype(jnp.float32)
    table[halo_rows + own_rows:, :] = high_ref[...].astype(jnp.float32)
    parts, nodes, part_width = mesh_all_ref.shape
    recv_terms_ref[...] = hidden_bias_ref[...] + sum(
        jnp.dot(
            mesh_all_ref[n],
            receiver_ref[n * part_width:(n + 1) * part_width, :],
            preferred_element_type=jnp.float32,
        )
        for n in range(parts)
    )
    total[...] = jnp.zeros_like(total)
    copy.wait()
    chunks = recv_row_ref.shape[1] // CHUNK
    width = recv_terms_ref.shape[1]

    def gather(chunk, held):
        base = chunk * CHUNK
        for i in range(CHUNK):
            held[pl.ds(i, 1), :] = (
                table[pl.ds(send_ref[base + i], 1), :]
                + recv_terms_ref[pl.ds(recv_ref[base + i], 1), :]
            )

    def add_up(chunk, held):
        lanes = pl.ds(pl.multiple_of(chunk * CHUNK, CHUNK), CHUNK)
        before = held[...] + lax.dot_general(
            features_ref[:, lanes],
            feature_weight_ref[...],
            (((0,), (0,)), ((), ())),
            preferred_element_type=jnp.float32,
        )
        hidden = silu(before).astype(jnp.bfloat16)
        ids = lax.broadcasted_iota(jnp.int32, (nodes, CHUNK), 0)
        one_hot = jnp.where(ids == recv_row_ref[:, lanes], 1.0, 0.0).astype(jnp.bfloat16)
        widened = jnp.concatenate([hidden, jnp.ones((CHUNK, width), jnp.bfloat16)], axis=1)
        total[...] += jnp.dot(one_hot, widened, preferred_element_type=jnp.float32)

    gather(0, even)

    def pair(n, carry):
        gather(2 * n + 1, odd)
        add_up(2 * n, even)
        gather(jnp.minimum(2 * n + 2, chunks - 1), even)
        add_up(2 * n + 1, odd)
        return carry

    lax.fori_loop(0, chunks // 2, pair, 0)
    out_ref[...] = total[:, :width]
    tally_ref[...] = total[:, width:]


def node_sums(
    send, recv, own, low, high, mesh_all, receiver_weight, hidden_bias, features, feature_weight
):
    edges = send.shape[0]
    parts, nodes, width = mesh_all.shape
    table_rows = own.shape[0] + 2 * low.shape[0]
    vmem = pl.BlockSpec(memory_space=pltpu.VMEM)
    smem = pl.BlockSpec(memory_space=pltpu.SMEM)
    hbm = pl.BlockSpec(memory_space=pl.ANY)
    return pl.pallas_call(
        edge_kernel,
        in_specs=[smem, smem, hbm] + [vmem] * 8,
        out_specs=[vmem, vmem],
        out_shape=[jax.ShapeDtypeStruct((nodes, width), jnp.float32)] * 2,
        scratch_shapes=[
            pltpu.VMEM((table_rows, width), jnp.float32),
            pltpu.VMEM((nodes, width), jnp.float32),
            pltpu.VMEM((CHUNK, width), jnp.float32),
            pltpu.VMEM((CHUNK, width), jnp.float32),
            pltpu.VMEM((nodes, 2 * width), jnp.float32),
            pltpu.SemaphoreType.DMA,
        ],
        compiler_params=pltpu.CompilerParams(vmem_limit_bytes=48 << 20),
        cost_estimate=pl.CostEstimate(
            flops=4 * edges * nodes * width,
            bytes_accessed=4 * table_rows * width,
            transcendentals=edges * width,
        ),
    )(send, recv, own, low, high, mesh_all, receiver_weight, hidden_bias.reshape(1, -1),
      recv.reshape(1, -1), features, feature_weight)


def tail_kernel(
    totals_ref,
    tally_ref,
    message_ref,
    message_bias_ref,
    latent_ref,
    gain_ref,
    shift_ref,
    out_ref,
    got,
    give,
    back,
    there_send,
    there_recv,
    back_send,
    back_recv,
):
    ch_count = lax.axis_size("ch")
    me = lax.axis_index("ch")
    parts, part, width = got.shape
    partners = [lax.rem(me + j, ch_count) for j in range(1, ch_count)]
    barrier = pltpu.get_barrier_semaphore()
    for partner in partners:
        pl.semaphore_signal(
            barrier, inc=1, device_id={"ch": partner}, device_id_type=pl.DeviceIdType.MESH
        )
    pl.semaphore_wait(barrier, ch_count - 1)

    def copy_to(source, target, sends, recvs, j, partner):
        return pltpu.make_async_remote_copy(
            src_ref=source,
            dst_ref=target.at[me],
            send_sem=sends.at[j],
            recv_sem=recvs.at[j],
            device_id={"ch": partner},
            device_id_type=pl.DeviceIdType.MESH,
        )

    there = [
        copy_to(totals_ref.at[partner], got, there_send, there_recv, j, partner)
        for j, partner in enumerate(partners)
    ]
    for copy in there:
        copy.start()
    got[me] = totals_ref[me]
    bias = tally_ref[me][:, :1] * message_bias_ref[...]
    for copy in there:
        copy.wait()
    aggregated = bias
    for n in range(parts):
        rest = got[n]
        for _ in range(3):
            piece = rest.astype(jnp.bfloat16)
            aggregated += jnp.dot(piece, message_ref[n], preferred_element_type=jnp.float32)
            rest = rest - piece.astype(jnp.float32)
    centre = jnp.mean(aggregated, axis=1, keepdims=True)
    spread = jnp.mean(jnp.square(aggregated - centre), axis=1, keepdims=True)
    normed = (aggregated - centre) * lax.rsqrt(spread + 1.0)
    for n in range(parts):
        give[n] = normed[:, n * width:(n + 1) * width]
    back[me] = give[me]
    returns = [
        copy_to(give.at[partner], back, back_send, back_recv, j, partner)
        for j, partner in enumerate(partners)
    ]
    for copy in returns:
        copy.start()
    for copy in returns:
        copy.wait()
    for n in range(parts):
        rows = slice(n * part, (n + 1) * part)
        out_ref[rows, :] = (
            latent_ref[rows, :].astype(jnp.float32) + back[n] * gain_ref[...] + shift_ref[...]
        ).astype(out_ref.dtype)


def finished(totals, tallies, message_all, message_bias, mesh_latent, norm_gain, norm_shift):
    nodes, width = mesh_latent.shape
    ch_count = lax.axis_size("ch")
    blocks = (ch_count, nodes // ch_count, width)
    vmem = pl.BlockSpec(memory_space=pltpu.VMEM)
    return pl.pallas_call(
        tail_kernel,
        in_specs=[vmem] * 7,
        out_specs=vmem,
        out_shape=jax.ShapeDtypeStruct((nodes, width), jnp.bfloat16),
        scratch_shapes=[pltpu.VMEM(blocks, jnp.float32)] * 3
        + [pltpu.SemaphoreType.DMA((ch_count - 1,))] * 4,
        compiler_params=pltpu.CompilerParams(
            vmem_limit_bytes=32 << 20, collective_id=1, has_side_effects=True
        ),
    )(totals.reshape(blocks), tallies.reshape(blocks), message_all, message_bias.reshape(1, -1),
      mesh_latent, norm_gain.reshape(1, -1), norm_shift.reshape(1, -1))


def on_device(
    grid_inputs,
    embed_weight,
    embed_bias,
    mesh_latent,
    edge_features,
    senders,
    receivers,
    sender_weight,
    receiver_weight,
    feature_weight,
    hidden_bias,
    message_weight,
    message_bias,
    norm_gain,
    norm_shift,
):
    lon_count = lax.axis_size("lon")
    lon_place = lax.axis_index("lon")
    columns = grid_inputs.shape[0] // LAT
    mesh_nodes = mesh_latent.shape[0]

    own, low, high, mesh_all, message_all = sender_terms(
        grid_inputs, embed_weight, embed_bias, sender_weight, mesh_latent, message_weight
    )
    grid_column = senders // LAT
    shifted = jnp.mod(grid_column - lon_place * columns + HALO, columns * lon_count)
    local_send = shifted * LAT + senders % LAT
    local_recv = receivers - lon_place * mesh_nodes
    pad = 16 - edge_features.shape[0]
    totals, tallies = node_sums(
        local_send, local_recv, own, low, high, mesh_all, receiver_weight, hidden_bias,
        jnp.pad(edge_features, ((0, pad), (0, 0))),
        jnp.pad(feature_weight, ((0, pad), (0, 0))),
    )
    return finished(
        totals, tallies, message_all, message_bias, mesh_latent, norm_gain, norm_shift
    )


def solution(mesh):
    return jax.shard_map(
        on_device,
        mesh=mesh,
        in_specs=(
            P("lon", None),
            P(),
            P(),
            P("lon", "ch"),
            P(None, "lon"),
            P("lon"),
            P("lon"),
            P(None, "ch"),
            P(None, "ch"),
            P(None, "ch"),
            P("ch"),
            P("ch", None),
            P(),
            P("ch"),
            P("ch"),
        ),
        out_specs=P("lon", "ch"),
        check_vma=False,
    )
```

profile of v0, /device:TPU:0, one launch (start us, length us, event | category | flops | bytes accessed | tf_op | source)
XLA Modules:
  0.0 115.3 jit_solution(16032474490628082832)
XLA Ops:
  0.0 0.7 pad.9.feature_weight_ref
  0.7 1.1 fusion.4
  1.8 1.0 pad.8.features_ref
  2.8 0.0 copy-start.5
  2.8 0.0 copy-start.6
  2.8 0.0 copy-start.1
  2.8 0.0 copy-start.2
  2.8 0.0 copy-start.3
  2.8 0.0 copy-start.4
  2.9 40.3 %shard_map.145 = (f32[28800,128]{1,0:T(8,128)}, bf16[2560,128]{1,0:T(8,128)(2,1)}, bf16[2560,128]{1,0:T(8,128)(2,1)}, bf16[4,640,128]{2,1,0:T(8,128)(2,1)}, bf16[4,128,512]{2,1,0:T(8,128)(2,1)}) custom-call(bf16[474,28800]{1,0:T(8,128)(2,1)} %bitcast.16, bf16[474,512]{1,0:T(8,128)(2,1)} %embed_ref.1, f32[1,512]{1,0:T(1,128)} %bitcast.17, ...), custom_call_target="tpu_custom_call" | custom-call | flops 17753702400 | bytes 42048000 | tf_op jit(solution)/shard_map/pallas_call | solution.py:140
  43.2 0.0 copy-start
  43.2 0.0 copy-done.5
  43.2 0.0 copy-done.6
  43.2 0.0 copy-start.7
  43.2 1.1 copy-done.7
  44.3 0.0 copy-start.8
  44.4 1.1 copy-done.8
  45.4 0.0 copy-start.9
  45.4 1.1 copy-done.9
  46.5 57.0 %shard_map.146 = (f32[640,128]{1,0:T(8,128)S(1)}, f32[640,128]{1,0:T(8,128)S(1)}) custom-call(s32[22528]{0:T(1024)S(1)} %get-tuple-element.19.send_ref, s32[22528]{0:T(1024)S(1)} %get-tuple-element.20.recv_ref, f32[28800,128]{1,0:T(8,128)} %get-tuple-element.12.own_ref, bf16[2560,128]{1,0:T(8,128)(2,1)S(1)} %copy-done.7, bf16[2560,128]{1,0:T(8,128)(2,1)S(1)} %copy-done.8, ...), custom_call_target="tpu_custom_call" | custom-call | flops 7381975040 | bytes 17367040 | tf_op jit(solution)/shard_map/pallas_call | solution.py:266
  103.5 0.0 copy-done.1
  103.6 0.0 copy-done.2
  103.6 0.0 copy-done.3
  103.6 0.0 copy-done.4
  103.6 0.0 copy-done
  103.6 11.0 %shard_map.147 = bf16[640,128]{1,0:T(8,128)(2,1)S(1)} custom-call(f32[4,160,128]{2,1,0:T(8,128)S(1)} %bitcast.9, f32[4,160,128]{2,1,0:T(8,128)S(1)} %bitcast.10, bf16[4,128,512]{2,1,0:T(8,128)(2,1)S(1)} %copy-done, f32[1,512]{1,0:T(1,128)S(1)} %bitcast.12, bf16[640,128]{1,0:T(8,128)(2,1)S(1)} %copy-done.1, f32[1,128]{1,0:T(1,128)S(1)} %bitcast.13, ...), custom_call_target="tpu_custom_call" | custom-call | tf_op jit(solution)/shard_map/pallas_call | solution.py:370
  114.6 0.7 copy.17
Async XLA Ops:
  2.8 40.4 %copy-start.5 = (bf16[512,128]{1,0:T(8,128)(2,1)S(1)}, bf16[512,128]{1,0:T(8,128)(2,1)}, u32[]{:S(2)}) copy-start(bf16[512,128]{1,0:T(8,128)(2,1)} %receiver_ref.1) | copy-start | bytes 393220
  2.8 40.4 %copy-start.6 = (f32[128]{0:T(128)S(1)}, f32[128]{0:T(128)}, u32[]{:S(2)}) copy-start(f32[128]{0:T(128)} %param.25) | copy-start | bytes 1540
  2.8 100.7 %copy-start.1 = (bf16[640,128]{1,0:T(8,128)(2,1)S(1)}, bf16[640,128]{1,0:T(8,128)(2,1)}, u32[]{:S(2)}) copy-start(bf16[640,128]{1,0:T(8,128)(2,1)} %latent_ref.1) | copy-start | bytes 491524
  2.8 100.7 %copy-start.2 = (f32[512]{0:T(512)S(1)}, f32[512]{0:T(512)}, u32[]{:S(2)}) copy-start(f32[512]{0:T(512)} %param.27) | copy-start | bytes 6148
  2.8 100.7 %copy-start.3 = (f32[128]{0:T(128)S(1)}, f32[128]{0:T(128)}, u32[]{:S(2)}) copy-start(f32[128]{0:T(128)} %param.28) | copy-start | bytes 1540
  2.8 100.7 %copy-start.4 = (f32[128]{0:T(128)S(1)}, f32[128]{0:T(128)}, u32[]{:S(2)}) copy-start(f32[128]{0:T(128)} %param.29) | copy-start | bytes 1540
  43.2 60.4 %copy-start = (bf16[4,128,512]{2,1,0:T(8,128)(2,1)S(1)}, bf16[4,128,512]{2,1,0:T(8,128)(2,1)}, u32[]{:S(2)}) copy-start(bf16[4,128,512]{2,1,0:T(8,128)(2,1)} %get-tuple-element.18.message_ref) | copy-start | bytes 1572868
  43.2 1.1 copy-start.7
  44.3 1.1 copy-start.8
  45.4 1.1 copy-start.9
where the time goes:
time: 117 us; the launch traced here: 115 us
  Pallas kernels  108 us (92%)
  local copies, waits for them, and re-layouts  5.7 us (5%)
    pallas_call x1, Pallas kernels, node_sums(): pl.pallas_call(edge_kernel, in_specs=[smem, smem, hbm] + [vmem] * 8, out_...  57 us
    pallas_call x1, Pallas kernels, sender_terms(): pl.pallas_call(functools.partial(dense_kernel, steps), grid=(steps,), in_...  40.3 us
    pallas_call x1, Pallas kernels, finished(): pl.pallas_call(tail_kernel, in_specs=[vmem] * 7, out_specs=vmem, out_shap...  11 us
    unnamed x21, local copies, waits for them, and re-layouts  4.02 us

commit v1 on v0

v1 whole, which is shorter than its diff:
```python
import functools

import jax
import jax.numpy as jnp
from jax import lax
from jax.experimental import pallas as pl
from jax.experimental.pallas import tpu as pltpu
from jax.sharding import PartitionSpec as P

LAT = 640
HALO = 4
UNIT = 512
WINDOW = 7
SLOTS = 8
LANES = 128
CHUNK = 256


def silu(v):
    half = 0.5 * v
    return half + half * jnp.tanh(half)


def pick_units(low_ref, high_ref, list_ref, columns, halo_turn):
    me = lax.axis_index("ch")
    ch_count = lax.axis_size("ch")
    units = low_ref.shape[0]
    one = lambda flag: jnp.where(flag, 1, 0)
    at_left = [one(low_ref[u] < HALO) for u in range(units)]
    at_right = [one(high_ref[u] >= HALO + columns) for u in range(units)]
    lefts, rights = sum(at_left), sum(at_right)
    inner_count = units - lefts - rights
    even_share = -(-units // ch_count)
    first = jnp.minimum(jnp.maximum(even_share - lefts, 0), inner_count)
    last = jnp.maximum(inner_count - jnp.maximum(even_share - rights, 0), first)
    middle = lambda k: first + lax.div((last - first) * (k - 1), ch_count - 2)
    begin = jnp.where(me == 0, 0, middle(me))
    end = jnp.where(me == ch_count - 1, inner_count, middle(me + 1))
    count, rank = jnp.int32(0), jnp.int32(0)
    for u in range(units):
        inner = 1 - at_left[u] - at_right[u]
        if halo_turn:
            mine = jnp.where(me == 0, at_left[u], 0) + jnp.where(
                me == ch_count - 1, at_right[u], 0
            )
        else:
            inside = jnp.logical_and(rank >= begin, rank < end)
            mine = jnp.where(inside, inner, 0)
        list_ref[count] = u
        count = count + mine
        rank = rank + inner
    return count


def gather_kernel(
    columns,
    halo_turn,
    low_ref,
    high_ref,
    send_ref,
    x_ref,
    halo_ref,
    embed_ref,
    bias_ref,
    out_ref,
    list_ref,
    events,
    event_at,
    held_column,
    index,
    points,
    table,
    even,
    odd,
    packed,
    index_sem,
    point_sem,
    out_sem,
):
    parts = out_ref.shape[1] // LANES
    unit = send_ref.shape[1]
    step = LAT * parts
    depth = points.shape[0]
    count = pick_units(low_ref, high_ref, list_ref, columns, halo_turn)

    for n in range(SLOTS):
        held_column[n] = -1

    def note_unit(n, total):
        u = list_ref[n]
        event_at[n] = total

        def note(column, total):
            slot = lax.rem(column, SLOTS)
            new = jnp.where(held_column[slot] == column, 0, 1)
            held_column[slot] = column
            events[total] = column
            return total + new

        return lax.fori_loop(low_ref[u], high_ref[u] + 1, note, total)

    total = lax.fori_loop(0, count, note_unit, jnp.int32(0))
    event_at[count] = total

    def fetch(event):
        column, slot = events[event], lax.rem(event, depth)

        def copy(source, place):
            start = pl.multiple_of(place * LAT, LANES)
            return pltpu.make_async_copy(
                source.at[:, pl.ds(start, LAT)], points.at[slot], point_sem.at[slot]
            )

        if not halo_turn:
            copy(x_ref, column - HALO).start()
            return
        last = column >= HALO + columns
        outside = jnp.logical_or(column < HALO, last)
        pl.when(outside)(
            lambda: copy(halo_ref, jnp.where(last, column - HALO - columns, column)).start()
        )
        pl.when(jnp.logical_not(outside))(lambda: copy(x_ref, column - HALO).start())

    def fetch_index(n):
        slot = lax.rem(n, 2)
        return pltpu.make_async_copy(
            send_ref.at[list_ref[n]], index.at[slot], index_sem.at[slot]
        )

    for event in range(depth):
        pl.when(event < total)(functools.partial(fetch, event))
    pl.when(count > 0)(lambda: fetch_index(0).start())

    def one_event(event, carry):
        slot = lax.rem(event, depth)
        pltpu.make_async_copy(
            x_ref.at[:, pl.ds(0, LAT)], points.at[slot], point_sem.at[slot]
        ).wait()
        before = lax.dot_general(
            points[slot], embed_ref[...], (((0,), (0,)), ((), ())),
            preferred_element_type=jnp.float32,
        ) + bias_ref[...]
        latent = silu(before)
        base = lax.rem(events[event], SLOTS) * step
        for j in range(parts):
            table[pl.ds(base + j, LAT, stride=parts), :] = latent[:, j * LANES:(j + 1) * LANES]
        pl.when(event + depth < total)(lambda: fetch(event + depth))
        return carry

    def gather(n, half, held):
        slot = lax.rem(n, 2)
        for i in range(CHUNK):
            place = pl.multiple_of(index[slot, half * CHUNK + i], parts)
            held[pl.ds(parts * i, parts), :] = table[pl.ds(place, parts), :]

    def leave(n, half, held):
        start = pl.multiple_of(list_ref[n] * unit + half * CHUNK, CHUNK)
        for j in range(parts):
            packed[half, :, j * LANES:(j + 1) * LANES] = (
                held[pl.ds(j, CHUNK, stride=parts), :].astype(jnp.bfloat16)
            )
        pltpu.make_async_copy(
            packed.at[half], out_ref.at[pl.ds(start, CHUNK), :], out_sem.at[half]
        ).start()

    def settle(half):
        pltpu.make_async_copy(
            packed.at[half], out_ref.at[pl.ds(0, CHUNK), :], out_sem.at[half]
        ).wait()

    def one_unit(n, carry):
        pl.when(n + 1 < count)(lambda: fetch_index(n + 1).start())
        lax.fori_loop(event_at[n], event_at[n + 1], one_event, 0)
        fetch_index(n).wait()
        for half in range(2):
            pl.when(n > 0)(functools.partial(settle, half))
        leave(jnp.maximum(n - 1, 0), 1, odd)
        gather(n, 0, even)
        leave(n, 0, even)
        gather(n, 1, odd)
        return carry

    lax.fori_loop(0, count, one_unit, 0)

    @pl.when(count > 0)
    def _():
        settle(1)
        leave(count - 1, 1, odd)
        for half in range(2):
            settle(half)


def gathered(low, high, send, points, halo, embed_weight, embed_bias, halo_turn):
    channels, width = embed_weight.shape
    columns = points.shape[1] // LAT
    parts = width // LANES
    units, unit = send.shape
    vmem = pl.BlockSpec(memory_space=pltpu.VMEM)
    smem = pl.BlockSpec(memory_space=pltpu.SMEM)
    hbm = pl.BlockSpec(memory_space=pl.ANY)
    return pl.pallas_call(
        functools.partial(gather_kernel, columns, halo_turn),
        in_specs=[smem, smem, hbm, hbm, hbm, vmem, vmem],
        out_specs=hbm,
        out_shape=jax.ShapeDtypeStruct((units * unit, width), jnp.bfloat16),
        scratch_shapes=[
            pltpu.SMEM((units + 1,), jnp.int32),
            pltpu.SMEM((units * WINDOW + 1,), jnp.int32),
            pltpu.SMEM((units + 1,), jnp.int32),
            pltpu.SMEM((SLOTS,), jnp.int32),
            pltpu.SMEM((2, unit), jnp.int32),
            pltpu.VMEM((4, channels, LAT), jnp.bfloat16),
            pltpu.VMEM((SLOTS * LAT * parts, LANES), jnp.float32),
            pltpu.VMEM((CHUNK * parts, LANES), jnp.float32),
            pltpu.VMEM((CHUNK * parts, LANES), jnp.float32),
            pltpu.VMEM((2, CHUNK, width), jnp.bfloat16),
            pltpu.SemaphoreType.DMA((2,)),
            pltpu.SemaphoreType.DMA((4,)),
            pltpu.SemaphoreType.DMA((2,)),
        ],
        compiler_params=pltpu.CompilerParams(vmem_limit_bytes=40 << 20),
        cost_estimate=pl.CostEstimate(
            flops=2 * units * unit * channels * width,
            bytes_accessed=units * unit * width,
            transcendentals=units * unit * width // 2,
        ),
    )(low, high, send, points, points if halo is None else halo,
      embed_weight, embed_bias.reshape(1, -1))


def edge_kernel(
    columns,
    halo_turn,
    rows,
    low_ref,
    high_ref,
    gathered_ref,
    recv_ref,
    recv_row_ref,
    features_ref,
    start_ref,
    *refs,
):
    ways = lax.axis_size("ch")
    pieces = refs[:ways]
    (out_ref, list_ref, index, sender_all, receiver_all, recv_terms, feature_all, even, odd,
     held, hidden, index_sem, sem) = refs[ways:]
    me = lax.axis_index("ch")
    nodes, width = out_ref.shape
    part = width // ways
    parts = width // LANES
    unit = recv_ref.shape[1]
    rings = index.shape[0]
    count = pick_units(low_ref, high_ref, list_ref, columns, halo_turn)

    def fetch(n):
        slot = lax.rem(n, 2)
        start = pl.multiple_of(list_ref[n] * unit, unit)
        return pltpu.make_async_copy(
            gathered_ref.at[pl.ds(start, unit), :], held.at[slot], sem.at[slot]
        )

    def fetch_index(n):
        slot = lax.rem(n, rings)
        return pltpu.make_async_copy(
            recv_ref.at[list_ref[n]], index.at[slot], index_sem.at[slot]
        )

    @pl.when(count > 0)
    def _():
        fetch(0).start()
        fetch_index(0).start()

    pl.when(count > 1)(lambda: fetch_index(1).start())
    at = [sum(rows[:n]) for n in range(len(rows) + 1)]
    for j, piece in enumerate(pieces):
        lanes = slice(j * part, (j + 1) * part)
        sender_all[:, lanes] = piece[at[0]:at[1], :]
        receiver_all[:, lanes] = piece[at[1]:at[2], :]
        feature_all[:, lanes] = piece[at[3]:at[4], :]
    terms = jnp.zeros((nodes, width), jnp.float32)
    for j, piece in enumerate(pieces):
        owner = jnp.bitwise_xor(me, j)
        terms += jnp.dot(
            piece[at[2]:at[3], :],
            receiver_all[pl.ds(pl.multiple_of(owner * part, part), part), :],
            preferred_element_type=jnp.float32,
        )
    for j in range(parts):
        recv_terms[pl.ds(j, nodes, stride=parts), :] = terms[:, j * LANES:(j + 1) * LANES]
    if halo_turn:
        out_ref[...] = start_ref[...]
    else:
        out_ref[...] = jnp.zeros_like(out_ref)

    def gather(n, half, rows_held):
        slot = lax.rem(n, rings)
        for i in range(CHUNK):
            place = pl.multiple_of(index[slot, half * CHUNK + i], parts)
            rows_held[pl.ds(parts * i, parts), :] = recv_terms[pl.ds(place, parts), :]

    def activate(n, half, rows_held):
        start = pl.multiple_of(list_ref[n] * unit + half * CHUNK, CHUNK)
        mine = slice(half * CHUNK, (half + 1) * CHUNK)
        before = jnp.dot(
            held[lax.rem(n, 2), mine, :], sender_all[...], preferred_element_type=jnp.float32
        )
        before += lax.dot_general(
            features_ref[:, pl.ds(start, CHUNK)], feature_all[...], (((0,), (0,)), ((), ())),
            preferred_element_type=jnp.float32,
        )
        for j in range(parts):
            lanes = slice(j * LANES, (j + 1) * LANES)
            hidden[mine, lanes] = silu(
                before[:, lanes] + rows_held[pl.ds(j, CHUNK, stride=parts), :]
            ).astype(jnp.bfloat16)

    @pl.when(count > 0)
    def _():
        fetch_index(0).wait()
        gather(0, 0, even)

    def one_unit(n, carry):
        after = n + 1 < count
        pl.when(after)(lambda: fetch(n + 1).start())
        pl.when(n + 2 < count)(lambda: fetch_index(n + 2).start())
        pl.when(after)(lambda: fetch_index(n + 1).wait())
        fetch(n).wait()
        gather(n, 1, odd)
        activate(n, 0, even)
        gather(jnp.where(after, n + 1, n), 0, even)
        activate(n, 1, odd)
        ids = recv_row_ref[:, pl.ds(pl.multiple_of(list_ref[n] * unit, unit), unit)]
        by_node = jnp.where(
            lax.broadcasted_iota(jnp.int32, (nodes, unit), 0) == ids, 1.0, 0.0
        ).astype(jnp.bfloat16)
        out_ref[...] += jnp.dot(by_node, hidden[...], preferred_element_type=jnp.float32)
        return carry

    lax.fori_loop(0, count, one_unit, 0)


def node_sums(low, high, found, recv, recv_row, features, start, pieces, rows, columns, nodes,
              halo_turn):
    edges, width = found.shape
    units, unit = recv.shape
    parts = width // LANES
    vmem = pl.BlockSpec(memory_space=pltpu.VMEM)
    smem = pl.BlockSpec(memory_space=pltpu.SMEM)
    hbm = pl.BlockSpec(memory_space=pl.ANY)
    return pl.pallas_call(
        functools.partial(edge_kernel, columns, halo_turn, rows),
        in_specs=[smem, smem, hbm, hbm, vmem, vmem, vmem] + [vmem] * len(pieces),
        out_specs=vmem,
        out_shape=jax.ShapeDtypeStruct((nodes, width), jnp.float32),
        scratch_shapes=[
            pltpu.SMEM((units + 1,), jnp.int32),
            pltpu.SMEM((4, unit), jnp.int32),
            pltpu.VMEM((width, width), jnp.bfloat16),
            pltpu.VMEM((width, width), jnp.bfloat16),
            pltpu.VMEM((nodes * parts, LANES), jnp.float32),
            pltpu.VMEM((rows[3], width), jnp.bfloat16),
            pltpu.VMEM((CHUNK * parts, LANES), jnp.float32),
            pltpu.VMEM((CHUNK * parts, LANES), jnp.float32),
            pltpu.VMEM((2, unit, width), jnp.bfloat16),
            pltpu.VMEM((unit, width), jnp.bfloat16),
            pltpu.SemaphoreType.DMA((4,)),
            pltpu.SemaphoreType.DMA((2,)),
        ],
        compiler_params=pltpu.CompilerParams(vmem_limit_bytes=40 << 20),
        cost_estimate=pl.CostEstimate(
            flops=edges * width * (width + 2 * nodes) // 2,
            bytes_accessed=edges * width // 2,
            transcendentals=edges * width // 4,
        ),
    )(low, high, found, recv, recv_row, features, start, *pieces)


def across(me, bit):
    return me + bit - 2 * bit * lax.rem(me // bit, 2)


def swapped(block, bit, width):
    parts = block.shape[1] // width
    return jnp.concatenate(
        [block[:, (n ^ bit) * width:((n ^ bit) + 1) * width] for n in range(parts)], axis=1
    )


def tail_kernel(
    rows,
    totals_ref,
    recv_ref,
    message_bias_ref,
    *refs,
):
    ch_count = lax.axis_size("ch")
    messages, pieces = refs[:ch_count], refs[ch_count:2 * ch_count]
    (out_ref, near, onward, far, normed, give, near_send, near_recv, far_send, far_recv,
     back_send, back_recv) = refs[2 * ch_count:]
    me = lax.axis_index("ch")
    parts, part, width = normed.shape
    beside, opposite = across(me, 1), across(me, 2)
    partners = [beside, opposite, across(opposite, 1)]
    barrier = pltpu.get_barrier_semaphore()
    for partner in partners:
        pl.semaphore_signal(
            barrier, inc=1, device_id={"ch": partner}, device_id_type=pl.DeviceIdType.MESH
        )
    pl.semaphore_wait(barrier, ch_count - 1)

    def copy_to(source, target, send, recv, partner):
        return pltpu.make_async_remote_copy(
            src_ref=source, dst_ref=target, send_sem=send, recv_sem=recv,
            device_id={"ch": partner}, device_id_type=pl.DeviceIdType.MESH,
        )

    nears = [
        copy_to(totals_ref.at[block], near.at[n], near_send.at[n], near_recv.at[n], beside)
        for n, block in enumerate((partners[2], beside))
    ]
    for copy in nears:
        copy.start()
    nears[0].wait()
    onward[...] = (totals_ref[opposite] + swapped(near[0], 1, width)).astype(onward.dtype)
    pass_on = copy_to(onward, far, far_send.at[0], far_recv.at[0], opposite)
    pass_on.start()

    def tally(n, counts):
        nodes_here = lax.broadcasted_iota(jnp.int32, (part, LANES), 0) + me * part
        for i in range(8):
            ids = recv_ref[pl.ds(n * 8 + i, 1), :]
            counts = counts + jnp.where(nodes_here == ids, 1.0, 0.0)
        return counts

    counts = lax.fori_loop(
        0, recv_ref.shape[0] // 8, tally, jnp.zeros((part, LANES), jnp.float32)
    )
    aggregated = jnp.sum(counts, axis=1, keepdims=True) * message_bias_ref[...]
    nears[1].wait()
    sums = totals_ref[me] + swapped(near[1], 1, width)
    pass_on.wait()
    sums = sums + swapped(far[...].astype(jnp.float32), 2, width)
    for n in range(parts):
        rest = sums[:, n * width:(n + 1) * width]
        for _ in range(3):
            piece = rest.astype(jnp.bfloat16)
            aggregated += jnp.dot(
                piece, messages[n][...], preferred_element_type=jnp.float32
            )
            rest = rest - piece.astype(jnp.float32)
    centre = jnp.mean(aggregated, axis=1, keepdims=True)
    spread = jnp.mean(jnp.square(aggregated - centre), axis=1, keepdims=True)
    result = (aggregated - centre) * lax.rsqrt(spread + 1.0)
    for n in range(parts):
        normed[n] = result[:, n * width:(n + 1) * width]
    at = [sum(rows[:n]) for n in range(len(rows) + 1)]
    mine = pl.ds(pl.multiple_of(me * part, part), part)
    returns = []
    for j in (3, 2, 1, 0):
        owner = ([me] + partners)[j]
        small = pieces[j][at[3]:at[4], :].astype(jnp.float32)
        gain = small[7:8] + small[8:9] + small[9:10]
        shift = small[10:11] + small[11:12] + small[12:13]
        latent = pieces[j][pl.ds(at[2] + pl.multiple_of(me * part, part), part), :]
        block = (latent.astype(jnp.float32) + normed[owner] * gain + shift).astype(out_ref.dtype)
        if j == 0:
            out_ref[mine, :] = block
            continue
        give[j - 1] = block
        copy = copy_to(
            give.at[j - 1], out_ref.at[mine, :], back_send.at[j - 1], back_recv.at[j - 1], owner
        )
        copy.start()
        returns.append(copy)
    for copy in returns:
        copy.wait()


def finished(totals, recv, messages, message_bias, pieces, rows, nodes):
    ch_count = lax.axis_size("ch")
    part = nodes // ch_count
    full = totals.shape[1]
    width = full // ch_count
    vmem = pl.BlockSpec(memory_space=pltpu.VMEM)
    return pl.pallas_call(
        functools.partial(tail_kernel, rows),
        in_specs=[vmem] * (3 + 2 * ch_count),
        out_specs=vmem,
        out_shape=jax.ShapeDtypeStruct((nodes, width), jnp.bfloat16),
        scratch_shapes=[
            pltpu.VMEM((2, part, full), jnp.float32),
            pltpu.VMEM((part, full), jnp.bfloat16),
            pltpu.VMEM((part, full), jnp.bfloat16),
            pltpu.VMEM((ch_count, part, width), jnp.float32),
            pltpu.VMEM((ch_count - 1, part, width), jnp.bfloat16),
            pltpu.SemaphoreType.DMA((2,)),
            pltpu.SemaphoreType.DMA((2,)),
            pltpu.SemaphoreType.DMA((1,)),
            pltpu.SemaphoreType.DMA((1,)),
            pltpu.SemaphoreType.DMA((ch_count - 1,)),
            pltpu.SemaphoreType.DMA((ch_count - 1,)),
        ],
        compiler_params=pltpu.CompilerParams(
            vmem_limit_bytes=32 << 20, collective_id=1, has_side_effects=True
        ),
    )(totals.reshape(ch_count, part, full), recv, message_bias.reshape(1, -1), *messages, *pieces)


def on_device(
    grid_inputs,
    embed_weight,
    embed_bias,
    mesh_latent,
    edge_features,
    senders,
    receivers,
    sender_weight,
    receiver_weight,
    feature_weight,
    hidden_bias,
    message_weight,
    message_bias,
    norm_gain,
    norm_shift,
):
    lon_count, ch_count = lax.axis_size("lon"), lax.axis_size("ch")
    lon_place, ch_place = lax.axis_index("lon"), lax.axis_index("ch")
    assert ch_count == 4
    columns = grid_inputs.shape[0] // LAT
    assert columns >= WINDOW
    mesh_nodes = mesh_latent.shape[0]
    width = embed_weight.shape[1]
    parts = width // LANES
    edges = senders.shape[0]
    unit = UNIT
    assert edges % unit == 0 and unit == 2 * CHUNK
    points = grid_inputs.T

    edge_start = jnp.where(ch_place == 0, (columns - HALO) * LAT, 0)
    edge_columns = lax.dynamic_slice(points, (0, edge_start), (points.shape[0], HALO * LAT))
    hops = []
    for i in range(lon_count):
        hops.append((i * ch_count, (i + 1) % lon_count * ch_count))
        hops.append(
            (i * ch_count + ch_count - 1, (i - 1) % lon_count * ch_count + ch_count - 1)
        )
    with jax.named_scope("halo_hop"):
        halo = lax.ppermute(edge_columns, ("lon", "ch"), hops)

    cut = lambda v: lax.reduce_precision(v, exponent_bits=8, mantissa_bits=7)

    def thirds(v):
        high = cut(v)
        mid = cut(v - high)
        return [high, mid, v - high - mid]

    components = edge_features.shape[0]
    singles = thirds(hidden_bias) + thirds(norm_gain) + thirds(norm_shift)
    pad = 16 - components - len(singles)
    small = jnp.concatenate(
        [
            feature_weight,
            jnp.stack(singles).astype(jnp.bfloat16),
            jnp.zeros((pad, feature_weight.shape[1]), jnp.bfloat16),
        ]
    )
    blocks = (sender_weight, receiver_weight, mesh_latent, small)
    rows = tuple(block.shape[0] for block in blocks)
    swap = lambda v: [v] + [
        lax.ppermute(v, "ch", [(i, i ^ j) for i in range(ch_count)]) for j in range(1, ch_count)
    ]
    with jax.named_scope("weights_hop"):
        pieces = swap(jnp.concatenate(blocks))
    with jax.named_scope("messages_hop"):
        messages = swap(message_weight)

    shifted = jnp.mod(senders // LAT - lon_place * columns + HALO, columns * lon_count)
    by_unit = shifted.reshape(-1, unit)
    low, high = jnp.min(by_unit, axis=1), jnp.max(by_unit, axis=1)
    send = ((shifted % SLOTS * LAT + senders % LAT) * parts).reshape(-1, unit)
    recv = receivers - lon_place * mesh_nodes
    features = jnp.concatenate(
        [
            edge_features,
            jnp.ones((3, edges), jnp.bfloat16),
            jnp.zeros((16 - components - 3, edges), jnp.bfloat16),
        ]
    )

    totals = jnp.zeros((8, LANES), jnp.float32)
    for halo_turn in (False, True):
        with jax.named_scope("halo_work" if halo_turn else "inner_work"):
            found = gathered(
                low, high, send, points, halo if halo_turn else None, embed_weight, embed_bias,
                halo_turn,
            )
            totals = node_sums(
                low, high, found, (recv * parts).reshape(-1, unit), recv.reshape(1, -1),
                features, totals, pieces, rows, columns, mesh_nodes, halo_turn,
            )
    return finished(
        totals, recv.reshape(-1, LANES), messages, message_bias, pieces, rows, mesh_nodes
    )


def solution(mesh):
    return jax.shard_map(
        on_device,
        mesh=mesh,
        in_specs=(
            P("lon", None),
            P(),
            P(),
            P("lon", "ch"),
            P(None, "lon"),
            P("lon"),
            P("lon"),
            P(None, "ch"),
            P(None, "ch"),
            P(None, "ch"),
            P("ch"),
            P("ch", None),
            P(),
            P("ch"),
            P("ch"),
        ),
        out_specs=P("lon", "ch"),
        check_vma=False,
    )
```

time: 117 us -> 95.7 us (0.82)
  Pallas kernels: 108 us -> 60.7 us
  starting transfers between devices: 0 us -> 14.1 us
  local copies, waits for them, and re-layouts: 5.7 us -> 14.1 us
  other arithmetic: 1.1 us -> 4.97 us
    pallas_call x3 -> x5, Pallas kernels: 108 us -> 60.7 us  [the longest x2 22.8 us: gathered(): pl.pallas_call(functools.partial(gather_kernel, columns, halo_turn), in_s...]
    ppermute x0 -> x7, starting transfers between devices: none -> 14.1 us  [the longest x6 10.5 us: on_device(): lax.ppermute(v, 'ch', [(i, i ^ j) for i in range(ch_count)])]
    concatenate x0 -> x3, local copies, waits for them, and re-layouts: none -> 3.69 us  [the longest x1 3.53 us: on_device(): pieces = swap(jnp.concatenate(blocks))]
    dynamic_slice x0 -> x1, local copies, waits for them, and re-layouts: none -> 3.42 us  [on_device(): lax.dynamic_slice(points, (0, edge_start), (points.shape[0], HALO * LAT))]
    reshape x0 -> x3, local copies, waits for them, and re-layouts: none -> 3.36 us  [the longest x1 1.54 us: on_device(): (recv * parts).reshape(-1, unit)]
    concatenate x0 -> x1, other arithmetic: none -> 1.97 us  [on_device(): jnp.concatenate([edge_features, jnp.ones((3, edges), jnp.bfloat16), jnp.z...]
    pad x2 -> x0, local copies, waits for them, and re-layouts: 1.68 us -> none  [the longest x1 1 us: on_device(): jnp.pad(edge_features, ((0, pad), (0, 0)))]
    mul x0 -> x2, other arithmetic: none -> 1.53 us  [the longest x1 0.86 us: on_device(): send = ((shifted % SLOTS * LAT + senders % LAT) * parts).reshape(-1, unit)]
  transfers between devices with their start and end apart: 0 -> 7, of which waited for: 0 -> 0; matrix products, arithmetic and copies ran while one was open for 0% -> 11% of each run, Pallas kernels for 0% -> 47%
where the time goes in v1:
time: 95.7 us; the launch traced here: 94 us
  Pallas kernels  60.7 us (63%)
  local copies, waits for them, and re-layouts  14.1 us (15%)
  starting transfers between devices  14.1 us (15%)
  other arithmetic  4.97 us (5%)
    pallas_call x2, Pallas kernels, gathered(): pl.pallas_call(functools.partial(gather_kernel, columns, halo_turn), in_s...  22.8 us
    pallas_call x2, Pallas kernels, node_sums(): pl.pallas_call(functools.partial(edge_kernel, columns, halo_turn, rows),...  21.3 us
    pallas_call x1, Pallas kernels, finished(): pl.pallas_call(functools.partial(tail_kernel, rows), in_specs=[vmem] * (3...  16.6 us
    ppermute x6, starting transfers between devices, on_device(): lax.ppermute(v, 'ch', [(i, i ^ j) for i in range(ch_count)])  10.5 us
    ppermute x1, starting transfers between devices, on_device(): halo = lax.ppermute(edge_columns, ('lon', 'ch'), hops)  3.61 us
    unnamed x17, local copies, waits for them, and re-layouts  3.57 us
    concatenate x1, local copies, waits for them, and re-layouts, on_device(): pieces = swap(jnp.concatenate(blocks))  3.53 us
    dynamic_slice x1, local copies, waits for them, and re-layouts, on_device(): lax.dynamic_slice(points, (0, edge_start), (points.shape[0], HALO * LAT))  3.42 us
  transfers between devices with their start and end apart: 7, of which 0 were waited for; matrix products, arithmetic and copies ran while one was open for 11% of the time, Pallas kernels for 47%

profile of v1, /device:TPU:0, one launch (start us, length us, event | category | flops | bytes accessed | tf_op | source)
XLA Modules:
  0.0 94.0 jit_solution(9856651594915071144)
XLA Ops:
  0.0 0.7 fusion.19
  0.7 0.7 fusion.11
  1.3 3.5 %concatenate.8.refs_0_.refs_4_ = bf16[1680,128]{1,0:T(8,128)(2,1)S(1)} concatenate(bf16[512,128]{1,0:T(8,128)(2,1)} %param.22, bf16[512,128]{1,0:T(8,128)(2,1)} %param.23, bf16[640,128]{1,0:T(8,128)(2,1)} %param.18, bf16[4,128]{1,0:T(4,128)(2,1)} %param.24, bf16[1,128]{1,0:T(2,128)(2,1)S(1)} %get-tuple-element.19, bf16[1,128]{1,0:T(2,128)(2,1)S(1)} %get-tuple-element.18, ...), dimensions={0} | concatenate | bytes 860160 | tf_op jit(solution)/shard_map/weights_hop/concatenate | solution.py:574
  4.9 0.5 collective-permute-start.1
  5.4 2.6 %collective-permute-start.2 = (bf16[1680,128]{1,0:T(8,128)(2,1)S(1)}, bf16[1680,128]{1,0:T(8,128)(2,1)}, u32[]{:S(2)}, u32[]{:S(2)}) collective-permute-start(bf16[1680,128]{1,0:T(8,128)(2,1)S(1)} %concatenate.8.refs_0_.refs_4_), channel_id=1, source_target_pairs={{0,2},{1,3},{2,0},{3,1},{4,6},{5,7},{6,4},{7,5},{8,10},{9,11},{10,... | collective-permute-start | bytes 1290248 | tf_op jit(solution)/shard_map/weights_hop/ppermute | solution.py:571
  8.0 0.0 collective-permute-start.3
  8.1 3.4 %dynamic-slice_bitcast_fusion = bf16[474,2560]{1,0:T(8,128)(2,1)} fusion(bf16[28800,474]{0,1:T(8,128)(2,1)} %param.15, s32[]{:T(128)S(6)} %select_n.29), kind=kLoop, calls=%fused_computation | loop fusion | bytes 4853764 | tf_op jit(solution)/shard_map/dynamic_slice | solution.py:541
  11.5 3.6 %collective-permute-start = (bf16[474,2560]{1,0:T(8,128)(2,1)}, bf16[474,2560]{1,0:T(8,128)(2,1)S(1)}, u32[]{:S(2)}, u32[]{:S(2)}) collective-permute-start(bf16[474,2560]{1,0:T(8,128)(2,1)} %dynamic-slice_bitcast_fusion), channel_id=1, source_target_pairs={{0,4},{3,31},{4,8},{7,3},{8,12},{11,7},{12,16},{15,11},{16,20},{19... | collective-permute-start | bytes 7280648 | tf_op jit(solution)/shard_map/halo_hop/ppermute | solution.py:549
  15.1 0.1 collective-permute-start.4
  15.2 0.9 fusion.6
  16.1 0.9 reshape.27
  17.0 0.1 fusion.20
  17.1 0.9 reshape.28.send_ref
  18.0 0.1 pad.1.clone
  18.1 0.1 pad.2.clone
  18.2 2.0 %maximum_maximum_fusion.features_ref = bf16[16,22528]{1,0:T(8,128)(2,1)} fusion(bf16[4,22528]{1,0:T(4,128)(2,1)} %param.19, bf16[16]{0:T(256)(128)(2,1)S(1)} %pad.2.clone, bf16[16]{0:T(256)(128)(2,1)S(1)} %pad.1.clone), kind=kLoop, calls=%fused_computation.1 | loop fusion | flops 2162688 | bytes 901184 | tf_op jit(solution)/shard_map/concatenate | solution.py:583
  20.1 16.9 %inner_work.2.gathered_ref = bf16[22528,512]{1,0:T(8,128)(2,1)} custom-call(s32[44]{0:T(128)S(1)} %get-tuple-element.6.low_ref, s32[44]{0:T(128)S(1)} %get-tuple-element.5.high_ref, s32[44,512]{1,0:T(8,128)S(1)} %reshape.28.send_ref, bf16[474,28800]{1,0:T(8,128)(2,1)} %bitcast.33, bf16[474,28800]{1,0:T(8,128)(2,1)} %bitcast.34, ...), custom_call_target="tpu_custom_call" | custom-call | flops 10934550528 | bytes 11534336 | tf_op jit(solution)/shard_map/inner_work/pallas_call | solution.py:201
  37.1 0.7 broadcast_multiply_fusion
  37.7 1.5 %reshape.30.recv_ref = s32[44,512]{1,0:T(8,128)} reshape(s32[22528]{0:T(1024)} %get-tuple-element.7) | data formatting | bytes 180224 | tf_op jit(solution)/shard_map/halo_work/reshape | solution.py:599
  39.3 0.0 collective-permute-done.1.refs_1_.refs_5_
  39.3 7.3 %collective-permute-start.5 = (bf16[128,512]{1,0:T(8,128)(2,1)}, bf16[128,512]{1,0:T(8,128)(2,1)S(1)}, u32[]{:S(2)}, u32[]{:S(2)}) collective-permute-start(bf16[128,512]{1,0:T(8,128)(2,1)} %refs_0_.1), channel_id=1, source_target_pairs={{0,2},{1,3},{2,0},{3,1},{4,6},{5,7},{6,4},{7,5},{8,10},{9,11},{10,... | collective-permute-start | bytes 393224 | tf_op jit(solution)/shard_map/messages_hop/ppermute | solution.py:571
  46.6 0.0 collective-permute-done.2.refs_2_.refs_6_
  46.6 0.0 collective-permute-start.6
  46.6 1.1 %copy-done.1 = bf16[16,22528]{1,0:T(8,128)(2,1)S(1)} copy-done((bf16[16,22528]{1,0:T(8,128)(2,1)S(1)}, bf16[16,22528]{1,0:T(8,128)(2,1)}, u32[]{:S(2)}) %copy-start.1) | copy-done | bytes 720920
  47.7 0.9 copy-done.2
  48.6 0.9 copy-done.3
  49.5 15.5 %inner_work.3.start_ref = f32[640,512]{1,0:T(8,128)S(1)} custom-call(s32[44]{0:T(128)S(1)} %get-tuple-element.6.low_ref, s32[44]{0:T(128)S(1)} %get-tuple-element.5.high_ref, bf16[22528,512]{1,0:T(8,128)(2,1)} %inner_work.2.gathered_ref, s32[44,512]{1,0:T(8,128)S(1)} %copy-done.3, s32[1,22528]{1,0:T(1,128)S(1)} %bitcast.27, bf16[16,22528]{1,0:T(8,128)(2,1)S(1)} %copy-done.1, ...), custom_call_target="tpu_custom_call" | custom-call | flops 10334765056 | bytes 5767168 | tf_op jit(solution)/shard_map/inner_work/pallas_call | solution.py:351
  65.0 5.9 %halo_work.2.gathered_ref = bf16[22528,512]{1,0:T(8,128)(2,1)} custom-call(s32[44]{0:T(128)S(1)} %get-tuple-element.6.low_ref, s32[44]{0:T(128)S(1)} %get-tuple-element.5.high_ref, s32[44,512]{1,0:T(8,128)S(1)} %reshape.28.send_ref, bf16[474,28800]{1,0:T(8,128)(2,1)} %bitcast.35, bf16[474,2560]{1,0:T(8,128)(2,1)S(1)} %collective-permute-done.halo_ref, ...), custom_call_target="tpu_custom_call" | custom-call | flops 10934550528 | bytes 11534336 | tf_op jit(solution)/shard_map/halo_work/pallas_call | solution.py:201
  70.9 0.0 copy-start.5
  70.9 5.8 %halo_work.3 = f32[640,512]{1,0:T(8,128)S(1)} custom-call(s32[44]{0:T(128)S(1)} %get-tuple-element.6.low_ref, s32[44]{0:T(128)S(1)} %get-tuple-element.5.high_ref, bf16[22528,512]{1,0:T(8,128)(2,1)} %halo_work.2.gathered_ref, s32[44,512]{1,0:T(8,128)S(1)} %copy-done.3, s32[1,22528]{1,0:T(1,128)S(1)} %bitcast.28, bf16[16,22528]{1,0:T(8,128)(2,1)S(1)} %copy-done.1, ...), custom_call_target="tpu_custom_call" | custom-call | flops 10334765056 | bytes 5767168 | tf_op jit(solution)/shard_map/halo_work/pallas_call | solution.py:351
  76.8 16.6 %shard_map.145 = bf16[640,128]{1,0:T(8,128)(2,1)S(1)} custom-call(f32[4,160,512]{2,1,0:T(8,128)S(1)} %bitcast.26, s32[176,128]{1,0:T(8,128)S(1)} %bitcast.29, f32[1,512]{1,0:T(1,128)S(1)} %bitcast.32, bf16[128,512]{1,0:T(8,128)(2,1)} %refs_0_.1, bf16[128,512]{1,0:T(8,128)(2,1)} %collective-permute-done.4.refs_1_, ...), custom_call_target="tpu_custom_call" | custom-call | tf_op jit(solution)/shard_map/pallas_call | solution.py:486
  93.4 0.7 copy.17
  (21 shorter events, 0.0 us)
Async XLA Ops:
  4.9 34.4 %collective-permute-start.1 = (bf16[1680,128]{1,0:T(8,128)(2,1)S(1)}, bf16[1680,128]{1,0:T(8,128)(2,1)}, u32[]{:S(2)}, u32[]{:S(2)}) collective-permute-start(bf16[1680,128]{1,0:T(8,128)(2,1)S(1)} %concatenate.8.refs_0_.refs_4_), channel_id=1, source_target_pairs={{0,1},{1,0},{2,3},{3,2},{4,5},{5,4},{6,7},{7,6},{8,9},{9,8},{10,11... | collective-permute-start | bytes 1290248 | tf_op jit(solution)/shard_map/weights_hop/ppermute | solution.py:571
  5.4 41.2 %collective-permute-start.2 = (bf16[1680,128]{1,0:T(8,128)(2,1)S(1)}, bf16[1680,128]{1,0:T(8,128)(2,1)}, u32[]{:S(2)}, u32[]{:S(2)}) collective-permute-start(bf16[1680,128]{1,0:T(8,128)(2,1)S(1)} %concatenate.8.refs_0_.refs_4_), channel_id=1, source_target_pairs={{0,2},{1,3},{2,0},{3,1},{4,6},{5,7},{6,4},{7,5},{8,10},{9,11},{10,... | collective-permute-start | bytes 1290248 | tf_op jit(solution)/shard_map/weights_hop/ppermute | solution.py:571
  8.0 38.6 %collective-permute-start.3 = (bf16[1680,128]{1,0:T(8,128)(2,1)S(1)}, bf16[1680,128]{1,0:T(8,128)(2,1)}, u32[]{:S(2)}, u32[]{:S(2)}) collective-permute-start(bf16[1680,128]{1,0:T(8,128)(2,1)S(1)} %concatenate.8.refs_0_.refs_4_), channel_id=1, source_target_pairs={{0,3},{1,2},{2,1},{3,0},{4,7},{5,6},{6,5},{7,4},{8,11},{9,10},{10,... | collective-permute-start | bytes 1290248 | tf_op jit(solution)/shard_map/weights_hop/ppermute | solution.py:571
  8.0 7.1 %copy-start.6 = (s32[22528]{0:T(1024)S(1)}, s32[22528]{0:T(1024)}, u32[]{:S(2)}) copy-start(s32[22528]{0:T(1024)} %param.20) | copy-start | bytes 270340
  8.1 12.1 %copy-start = (bf16[474,512]{1,0:T(8,128)(2,1)S(1)}, bf16[474,512]{1,0:T(8,128)(2,1)}, u32[]{:S(2)}) copy-start(bf16[474,512]{1,0:T(8,128)(2,1)} %embed_ref.3) | copy-start | bytes 1456132
  8.1 12.1 %copy-start.4 = (f32[512]{0:T(512)S(1)}, f32[512]{0:T(512)}, u32[]{:S(2)}) copy-start(f32[512]{0:T(512)} %param.17) | copy-start | bytes 6148
  11.5 53.6 %collective-permute-start = (bf16[474,2560]{1,0:T(8,128)(2,1)}, bf16[474,2560]{1,0:T(8,128)(2,1)S(1)}, u32[]{:S(2)}, u32[]{:S(2)}) collective-permute-start(bf16[474,2560]{1,0:T(8,128)(2,1)} %dynamic-slice_bitcast_fusion), channel_id=1, source_target_pairs={{0,4},{3,31},{4,8},{7,3},{8,12},{11,7},{12,16},{15,11},{16,20},{19... | collective-permute-start | bytes 7280648 | tf_op jit(solution)/shard_map/halo_hop/ppermute | solution.py:549
  15.1 61.7 %collective-permute-start.4 = (bf16[128,512]{1,0:T(8,128)(2,1)}, bf16[128,512]{1,0:T(8,128)(2,1)}, u32[]{:S(2)}, u32[]{:S(2)}) collective-permute-start(bf16[128,512]{1,0:T(8,128)(2,1)} %refs_0_.1), channel_id=1, source_target_pairs={{0,1},{1,0},{2,3},{3,2},{4,5},{5,4},{6,7},{7,6},{8,9},{9,8},{10,11... | collective-permute-start | bytes 393224 | tf_op jit(solution)/shard_map/messages_hop/ppermute | solution.py:571
  20.1 16.9 %copy-start.7 = (s32[22528]{0:T(1024)S(1)}, s32[22528]{0:T(1024)}, u32[]{:S(2)}) copy-start(s32[22528]{0:T(1024)} %param.21) | copy-start | bytes 270340
  39.3 37.5 %collective-permute-start.5 = (bf16[128,512]{1,0:T(8,128)(2,1)}, bf16[128,512]{1,0:T(8,128)(2,1)S(1)}, u32[]{:S(2)}, u32[]{:S(2)}) collective-permute-start(bf16[128,512]{1,0:T(8,128)(2,1)} %refs_0_.1), channel_id=1, source_target_pairs={{0,2},{1,3},{2,0},{3,1},{4,6},{5,7},{6,4},{7,5},{8,10},{9,11},{10,... | collective-permute-start | bytes 393224 | tf_op jit(solution)/shard_map/messages_hop/ppermute | solution.py:571
  46.6 30.2 %collective-permute-start.6 = (bf16[128,512]{1,0:T(8,128)(2,1)}, bf16[128,512]{1,0:T(8,128)(2,1)S(1)}, u32[]{:S(2)}, u32[]{:S(2)}) collective-permute-start(bf16[128,512]{1,0:T(8,128)(2,1)} %refs_0_.1), channel_id=1, source_target_pairs={{0,3},{1,2},{2,1},{3,0},{4,7},{5,6},{6,5},{7,4},{8,11},{9,10},{10,... | collective-permute-start | bytes 393224 | tf_op jit(solution)/shard_map/messages_hop/ppermute | solution.py:571
  46.6 1.1 %copy-start.1 = (bf16[16,22528]{1,0:T(8,128)(2,1)S(1)}, bf16[16,22528]{1,0:T(8,128)(2,1)}, u32[]{:S(2)}) copy-start(bf16[16,22528]{1,0:T(8,128)(2,1)} %maximum_maximum_fusion.features_ref) | copy-start | bytes 2162692
  47.7 0.9 copy-start.2
  48.6 0.9 copy-start.3
  70.9 5.9 %copy-start.5 = (f32[512]{0:T(512)S(1)}, f32[512]{0:T(512)}, u32[]{:S(2)}) copy-start(f32[512]{0:T(512)} %param.27) | copy-start | bytes 6148

commit v2 on v1

v2 whole, which is shorter than its diff:
```python
import functools

import jax
import jax.numpy as jnp
from jax import lax
from jax.experimental import pallas as pl
from jax.experimental.pallas import tpu as pltpu
from jax.sharding import PartitionSpec as P


LAT = 640
HALO = 4
UNIT = 512
WINDOW = 7
SLOTS = 8
PARTS = 4
LANES = 128
CHUNK = 256


def silu_of_double(half):
    return half + half * jnp.tanh(half)


def low_of(bounds_ref, u):
    return bounds_ref[0, u * (UNIT // LANES)]


def high_of(bounds_ref, u):
    return bounds_ref[1, u * (UNIT // LANES)]


def pick_units(bounds_ref, list_ref, units, columns, halo_turn):
    me = lax.axis_index("ch")
    ch_count = lax.axis_size("ch")
    one = lambda flag: jnp.where(flag, 1, 0)
    at_left = [one(low_of(bounds_ref, u) < HALO) for u in range(units)]
    at_right = [one(high_of(bounds_ref, u) >= HALO + columns) for u in range(units)]
    lefts, rights = sum(at_left), sum(at_right)
    inner_count = units - lefts - rights
    end_share = -(-units // ch_count)
    first = jnp.minimum(jnp.maximum(end_share - lefts, 0), inner_count)
    last = jnp.maximum(inner_count - jnp.maximum(end_share - rights, 0), first)
    middle = lambda k: first + lax.div((last - first) * (k - 1), ch_count - 2)
    begin = jnp.where(me == 0, 0, middle(me))
    end = jnp.where(me == ch_count - 1, inner_count, middle(me + 1))
    first_turn = -(-units * 5 // (8 * ch_count))
    count, rank = jnp.int32(0), jnp.int32(0)
    for u in range(units):
        inner = 1 - at_left[u] - at_right[u]
        if halo_turn:
            inside = jnp.logical_and(rank >= begin + first_turn, rank < end)
            at_mine = jnp.where(me == 0, at_left[u], 0) + jnp.where(
                me == ch_count - 1, at_right[u], 0
            )
            mine = jnp.where(inside, inner, at_mine)
        else:
            inside = jnp.logical_and(
                rank >= begin, rank < jnp.minimum(begin + first_turn, end)
            )
            mine = jnp.where(inside, inner, 0)
        list_ref[count] = u
        count = count + mine
        rank = rank + inner
    return count


def spread(ref, ids):
    for n in range(ids.shape[0] // 8):
        tile = ids[8 * n:8 * n + 8]
        ref[16 * n:16 * n + 8, :] = tile
        ref[16 * n + 8:16 * n + 16, :] = pltpu.roll(tile, 4, 0)


def prepare_kernel(
    columns,
    x_ref,
    *refs,
):
    sources, refs = refs[:10], refs[10:]
    (edge_ref, packed_ref, send_ref, recv_ref, place_ref, bounds_ref, buffer, packed,
     senders_ref, receivers_ref, feature_ref, bias_ref, gain_ref, shift_ref,
     in_sem, out_sem, pack_sem, source_sem) = refs
    lon_count = lax.axis_size("lon")
    lon_place, ch_place = lax.axis_index("lon"), lax.axis_index("ch")
    start = jnp.where(ch_place == 0, (columns - HALO) * LAT, 0)
    takes = [
        pltpu.make_async_copy(
            x_ref.at[:, pl.ds(pl.multiple_of(start + n * LAT, LANES), LAT)],
            buffer.at[n],
            in_sem.at[n],
        )
        for n in range(HALO)
    ]
    gives = [
        pltpu.make_async_copy(
            buffer.at[n], edge_ref.at[:, pl.ds(n * LAT, LAT)], out_sem.at[n]
        )
        for n in range(HALO)
    ]
    targets = [senders_ref, receivers_ref]
    row = 0
    for ref in sources[2:5]:
        targets.append(packed.at[pl.ds(row, ref.shape[0]), :])
        row += ref.shape[0]
    targets += [feature_ref, bias_ref, gain_ref, shift_ref]
    loads = [
        pltpu.make_async_copy(source, target, source_sem.at[n])
        for n, (source, target) in enumerate(zip(sources, targets))
    ]
    tall, part = sources[9].shape[0], packed.shape[1]
    loads += [
        pltpu.make_async_copy(
            sources[9].at[:, pl.ds(n * part, part)],
            packed.at[pl.ds(row + 16 + n * tall, tall), :],
            source_sem.at[9 + n],
        )
        for n in range(sources[9].shape[1] // part)
    ]
    for copy in takes + loads:
        copy.start()
    for copy in loads:
        copy.wait()
    singles = [feature_ref[...].astype(jnp.float32)]
    for ref in (bias_ref, gain_ref, shift_ref):
        rest = ref[...]
        for _ in range(3):
            high = rest.astype(jnp.bfloat16).astype(jnp.float32)
            singles.append(high)
            rest = rest - high
    used = feature_ref.shape[0] + len(singles) - 1
    singles.append(jnp.zeros((16 - used, singles[0].shape[1]), jnp.float32))
    packed[row:row + 16, :] = jnp.concatenate(singles).astype(jnp.bfloat16)
    pack = pltpu.make_async_copy(packed, packed_ref, pack_sem)
    pack.start()

    senders = senders_ref[...]
    column = lax.shift_right_logical(
        lax.shift_right_logical(senders, 7) * 52429, 18
    )
    latitude = senders - column * LAT
    total = columns * lon_count
    column = column - lon_place * columns + HALO
    column = jnp.where(column < 0, column + total, column)
    column = jnp.where(column >= total, column - total, column)
    parts = PARTS
    spread(send_ref, (jnp.bitwise_and(column, SLOTS - 1) * LAT + latitude) * parts)
    recv = receivers_ref[...] - lon_place * sources[4].shape[0]
    recv_ref[...] = recv
    spread(place_ref, recv * parts)
    tall = -(-senders.shape[0] // LANES) * LANES
    for n, (pick, near, fill) in enumerate(
        ((jnp.min, jnp.minimum, total), (jnp.max, jnp.maximum, 0))
    ):
        best = column
        for shift in (1, 2):
            best = near(best, pltpu.roll(best, best.shape[0] - shift, 0))
        best = jnp.concatenate(
            [best, jnp.full((tall - best.shape[0], LANES), fill, jnp.int32)]
        )
        bounds_ref[n:n + 1, :] = pick(jnp.transpose(best), axis=0, keepdims=True)
    for take, give in zip(takes, gives):
        take.wait()
        give.start()
    for give in gives:
        give.wait()
    pack.wait()


def prepared(points, senders, receivers, sender_weight, receiver_weight, mesh_latent,
             feature_weight, hidden_bias, norm_gain, norm_shift, message_weight):
    columns = points.shape[1] // LAT
    assert LAT == 5 * LANES and lax.axis_size("lon") * points.shape[1] // LANES < 40960
    rows = senders.shape[0] // LANES
    part = sender_weight.shape[1]
    packed_rows = (
        2 * sender_weight.shape[0] + receiver_weight.shape[0] + mesh_latent.shape[0] + 16
    )
    vmem = pl.BlockSpec(memory_space=pltpu.VMEM)
    hbm = pl.BlockSpec(memory_space=pltpu.HBM)
    ids = jax.ShapeDtypeStruct((rows, LANES), jnp.int32)
    wide_ids = jax.ShapeDtypeStruct((2 * rows, LANES), jnp.int32)
    assert rows % 8 == 0 and UNIT == 4 * LANES
    return pl.pallas_call(
        functools.partial(prepare_kernel, columns),
        in_specs=[hbm] * 11,
        out_specs=[hbm, hbm, vmem, vmem, vmem, vmem],
        out_shape=[
            jax.ShapeDtypeStruct((points.shape[0], HALO * LAT), points.dtype),
            jax.ShapeDtypeStruct((packed_rows, part), jnp.bfloat16),
            wide_ids,
            ids,
            wide_ids,
            jax.ShapeDtypeStruct((2, -(-rows // LANES) * LANES), jnp.int32),
        ],
        scratch_shapes=[
            pltpu.VMEM((HALO, points.shape[0], LAT), points.dtype),
            pltpu.VMEM((packed_rows, part), jnp.bfloat16),
            pltpu.VMEM((rows, LANES), jnp.int32),
            pltpu.VMEM((rows, LANES), jnp.int32),
            pltpu.VMEM(feature_weight.shape, jnp.bfloat16),
            pltpu.VMEM((1, part), jnp.float32),
            pltpu.VMEM((1, part), jnp.float32),
            pltpu.VMEM((1, part), jnp.float32),
            pltpu.SemaphoreType.DMA((HALO,)),
            pltpu.SemaphoreType.DMA((HALO,)),
            pltpu.SemaphoreType.DMA,
            pltpu.SemaphoreType.DMA((9 + PARTS,)),
        ],
        compiler_params=pltpu.CompilerParams(vmem_limit_bytes=63 << 20),
    )(points, senders.reshape(rows, LANES), receivers.reshape(rows, LANES), sender_weight,
      receiver_weight, mesh_latent, feature_weight, hidden_bias.reshape(1, -1),
      norm_gain.reshape(1, -1), norm_shift.reshape(1, -1), message_weight)


def index_rows(u):
    return pl.ds(pl.multiple_of(u * 8, 8), 8)


def gather_kernel(
    columns,
    halo_turn,
    bounds_ref,
    send_ref,
    x_ref,
    halo_ref,
    embed_ref,
    bias_ref,
    out_ref,
    list_ref,
    events,
    event_at,
    held_column,
    index_even,
    index_odd,
    points,
    table,
    even,
    odd,
    packed,
    embed_half,
    index_sem,
    point_sem,
    out_sem,
):
    index = (index_even, index_odd)
    parts = out_ref.shape[1] // LANES
    unit = UNIT
    step = LAT * parts
    depth = points.shape[0]
    count = pick_units(bounds_ref, list_ref, list_ref.shape[0] - 1, columns, halo_turn)

    embed_half[...] = embed_ref[...] * jnp.bfloat16(0.5)
    for n in range(SLOTS):
        held_column[n] = -1

    def note_unit(n, total):
        u = list_ref[n]
        event_at[n] = total

        def note(column, total):
            slot = lax.rem(column, SLOTS)
            new = jnp.where(held_column[slot] == column, 0, 1)
            held_column[slot] = column
            events[total] = column
            return total + new

        return lax.fori_loop(
            low_of(bounds_ref, u), high_of(bounds_ref, u) + 1, note, total
        )

    total = lax.fori_loop(0, count, note_unit, jnp.int32(0))
    event_at[count] = total

    def fetch(event):
        column, slot = events[event], lax.rem(event, depth)

        def copy(source, place):
            start = pl.multiple_of(place * LAT, LANES)
            return pltpu.make_async_copy(
                source.at[:, pl.ds(start, LAT)], points.at[slot], point_sem.at[slot]
            )

        if not halo_turn:
            copy(x_ref, column - HALO).start()
            return
        last = column >= HALO + columns
        outside = jnp.logical_or(column < HALO, last)
        pl.when(outside)(
            lambda: copy(halo_ref, jnp.where(last, column - HALO - columns, column)).start()
        )
        pl.when(jnp.logical_not(outside))(lambda: copy(x_ref, column - HALO).start())

    def fetch_index(n, slot):
        return pltpu.make_async_copy(
            send_ref.at[index_rows(list_ref[n]), :], index[slot], index_sem.at[slot]
        )

    for event in range(depth):
        pl.when(event < total)(functools.partial(fetch, event))
    for n in range(2):
        pl.when(n < count)(lambda n=n: fetch_index(n, n).start())

    def one_event(event, carry):
        slot = lax.rem(event, depth)
        pltpu.make_async_copy(
            x_ref.at[:, pl.ds(0, LAT)], points.at[slot], point_sem.at[slot]
        ).wait()
        before = lax.dot_general(
            points[slot], embed_half[...], (((0,), (0,)), ((), ())),
            preferred_element_type=jnp.float32,
        ) + 0.5 * bias_ref[...]
        latent = silu_of_double(before)
        base = lax.rem(events[event], SLOTS) * step
        for j in range(parts):
            table[pl.ds(base + j, LAT, stride=parts), :] = latent[:, j * LANES:(j + 1) * LANES]
        pl.when(event + depth < total)(lambda: fetch(event + depth))
        return carry

    def gather(slot, half, held):
        row = half * (CHUNK // LANES)
        for i in range(CHUNK):
            place = pl.multiple_of(index[slot][row + i // LANES, i % LANES], parts)
            held[pl.ds(parts * i, parts), :] = table[pl.ds(place, parts), :]

    def leave(start, slot, held):
        for j in range(parts):
            packed[slot, :, j * LANES:(j + 1) * LANES] = (
                held[pl.ds(j, CHUNK, stride=parts), :].astype(jnp.bfloat16)
            )
        pltpu.make_async_copy(
            packed.at[slot],
            out_ref.at[pl.ds(pl.multiple_of(start, CHUNK), CHUNK), :],
            out_sem.at[slot],
        ).start()

    def settle(slot):
        pltpu.make_async_copy(
            packed.at[slot], out_ref.at[pl.ds(0, CHUNK), :], out_sem.at[slot]
        ).wait()

    spare = out_ref.shape[0] - CHUNK

    def second_half(n):
        earlier = list_ref[jnp.maximum(n - 1, 0)] * unit + CHUNK
        return jnp.where(n > 0, earlier, spare)

    def one_unit(n, turn):
        lax.fori_loop(event_at[n], event_at[n + 1], one_event, 0)
        fetch_index(n, turn).wait()
        for slot in (turn, 2 + turn):
            pl.when(n > 1)(functools.partial(settle, slot))
        leave(second_half(n), 2 + turn, odd)
        gather(turn, 0, even)
        leave(list_ref[n] * unit, turn, even)
        gather(turn, 1, odd)
        pl.when(n + 2 < count)(lambda: fetch_index(n + 2, turn).start())

    def two_units(m, carry):
        one_unit(2 * m, 0)
        pl.when(2 * m + 1 < count)(lambda: one_unit(2 * m + 1, 1))
        return carry

    lax.fori_loop(0, (count + 1) // 2, two_units, 0)

    @pl.when(count > 0)
    def _():
        turn = lax.rem(count, 2)
        for slot in (turn, 2 + turn):
            pl.when(count > 1)(functools.partial(settle, slot))
        leave(second_half(count), 2 + turn, odd)
        settle(2 + turn)
        for slot in (1 - turn, 3 - turn):
            settle(slot)


def gathered(bounds, send, points, halo, embed_weight, embed_bias, halo_turn):
    channels, width = embed_weight.shape
    columns = points.shape[1] // LAT
    parts = width // LANES
    unit = UNIT
    units = send.shape[0] // 8
    vmem = pl.BlockSpec(memory_space=pltpu.VMEM)
    smem = pl.BlockSpec(memory_space=pltpu.SMEM)
    hbm = pl.BlockSpec(memory_space=pltpu.HBM)
    return pl.pallas_call(
        functools.partial(gather_kernel, columns, halo_turn),
        in_specs=[smem, hbm, hbm, hbm, vmem, vmem],
        out_specs=hbm,
        out_shape=jax.ShapeDtypeStruct((units * unit + CHUNK, width), jnp.bfloat16),
        scratch_shapes=[
            pltpu.SMEM((units + 1,), jnp.int32),
            pltpu.SMEM((units * WINDOW + 1,), jnp.int32),
            pltpu.SMEM((units + 1,), jnp.int32),
            pltpu.SMEM((SLOTS,), jnp.int32),
            pltpu.SMEM((8, LANES), jnp.int32),
            pltpu.SMEM((8, LANES), jnp.int32),
            pltpu.VMEM((6, channels, LAT), jnp.bfloat16),
            pltpu.VMEM((SLOTS * LAT * parts, LANES), jnp.float32),
            pltpu.VMEM((CHUNK * parts, LANES), jnp.float32),
            pltpu.VMEM((CHUNK * parts, LANES), jnp.float32),
            pltpu.VMEM((4, CHUNK, width), jnp.bfloat16),
            pltpu.VMEM((channels, width), jnp.bfloat16),
            pltpu.SemaphoreType.DMA((2,)),
            pltpu.SemaphoreType.DMA((6,)),
            pltpu.SemaphoreType.DMA((4,)),
        ],
        compiler_params=pltpu.CompilerParams(vmem_limit_bytes=40 << 20),
        cost_estimate=pl.CostEstimate(
            flops=2 * units * unit * channels * width,
            bytes_accessed=units * unit * width,
            transcendentals=units * unit * width // 2,
        ),
    )(bounds, send, points, points if halo is None else halo,
      embed_weight, embed_bias.reshape(1, -1))


def edge_kernel(
    columns,
    halo_turn,
    rows,
    bounds_ref,
    gathered_ref,
    place_ref,
    recv_ref,
    features_ref,
    start_ref,
    *refs,
):
    ways = lax.axis_size("ch")
    pieces = refs[:ways]
    (out_ref, list_ref, index, sender_all, receiver_all, recv_terms, feature_all, even, odd,
     held, hidden, index_sem, sem) = refs[ways:]
    me = lax.axis_index("ch")
    nodes, width = out_ref.shape
    part = width // ways
    parts = width // LANES
    unit = UNIT
    rings = index.shape[0]
    count = pick_units(bounds_ref, list_ref, list_ref.shape[0] - 1, columns, halo_turn)

    def fetch(n):
        slot = lax.rem(n, rings)
        start = pl.multiple_of(list_ref[n] * unit, unit)
        return pltpu.make_async_copy(
            gathered_ref.at[pl.ds(start, unit), :], held.at[slot], sem.at[slot]
        )

    def fetch_index(n):
        slot = lax.rem(n, rings)
        return pltpu.make_async_copy(
            place_ref.at[index_rows(list_ref[n]), :], index.at[slot], index_sem.at[slot]
        )

    def fetch_both(n):
        fetch_index(n).start()
        fetch(n).start()

    for n in range(rings - 2):
        pl.when(n < count)(functools.partial(fetch_both, n))
    at = [sum(rows[:n]) for n in range(len(rows) + 1)]
    for j, piece in enumerate(pieces):
        lanes = slice(j * part, (j + 1) * part)
        sender_all[:, lanes] = piece[at[0]:at[1], :] * jnp.bfloat16(0.5)
        receiver_all[:, lanes] = piece[at[1]:at[2], :]
        feature_all[:, lanes] = piece[at[3]:at[4], :] * jnp.bfloat16(0.5)
    components = features_ref.shape[0]
    singles = jnp.concatenate([piece[at[3]:at[4], :] for piece in pieces], axis=1)
    singles = singles.astype(jnp.float32)
    terms = jnp.broadcast_to(
        singles[components:components + 1] + singles[components + 1:components + 2]
        + singles[components + 2:components + 3],
        (nodes, width),
    )
    for j, piece in enumerate(pieces):
        owner = jnp.bitwise_xor(me, j)
        terms += jnp.dot(
            piece[at[2]:at[3], :],
            receiver_all[pl.ds(pl.multiple_of(owner * part, part), part), :],
            preferred_element_type=jnp.float32,
        )
    for j in range(parts):
        recv_terms[pl.ds(j, nodes, stride=parts), :] = (
            0.5 * terms[:, j * LANES:(j + 1) * LANES]
        )
    if halo_turn:
        out_ref[...] = start_ref[...]
    else:
        out_ref[...] = jnp.zeros_like(out_ref)

    def gather(n, rows_held):
        slot = lax.rem(n, rings)
        for i in range(unit):
            place = pl.multiple_of(index[slot, i // LANES, i % LANES], parts)
            rows_held[pl.ds(parts * i, parts), :] = recv_terms[pl.ds(place, parts), :]

    def activate(n, turn, rows_held):
        start = pl.multiple_of(list_ref[n] * unit, unit)
        mine = slice(turn * unit, (turn + 1) * unit)
        before = jnp.dot(
            held[lax.rem(n, rings)], sender_all[...], preferred_element_type=jnp.float32
        )
        before += lax.dot_general(
            features_ref[:, pl.ds(start, unit)], feature_all[:components, :],
            (((0,), (0,)), ((), ())),
            preferred_element_type=jnp.float32,
        )
        for j in range(parts):
            lanes = slice(j * LANES, (j + 1) * LANES)
            hidden[mine, lanes] = silu_of_double(
                before[:, lanes] + rows_held[pl.ds(j, unit, stride=parts), :]
            ).astype(jnp.bfloat16)

    def add_up(first, number):
        each = lax.broadcasted_iota(jnp.int32, (nodes, LANES), 0)
        by_node = jnp.concatenate(
            [
                jnp.where(
                    each == recv_ref[pl.ds(list_ref[first + n] * (unit // LANES) + b, 1), :],
                    1.0,
                    0.0,
                )
                for n in range(number)
                for b in range(unit // LANES)
            ],
            axis=1,
        ).astype(jnp.bfloat16)
        out_ref[...] += jnp.dot(
            by_node, hidden[:number * unit, :], preferred_element_type=jnp.float32
        )

    @pl.when(count > 0)
    def _():
        fetch_index(0).wait()
        gather(0, even)

    def pair(m, carry):
        first, second = 2 * m, 2 * m + 1
        after = second + 1 < count
        for n in (first, second):
            pl.when(n + rings - 2 < count)(functools.partial(fetch_both, n + rings - 2))
        fetch_index(second).wait()
        fetch(first).wait()
        gather(second, odd)
        activate(first, 0, even)
        pl.when(after)(lambda: fetch_index(second + 1).wait())
        fetch(second).wait()
        gather(jnp.where(after, second + 1, second), even)
        activate(second, 1, odd)
        add_up(first, 2)
        return carry

    lax.fori_loop(0, count // 2, pair, 0)

    @pl.when(lax.rem(count, 2) == 1)
    def _():
        fetch(count - 1).wait()
        activate(count - 1, 0, even)
        add_up(count - 1, 1)


def node_sums(bounds, found, place, recv, features, start, pieces, rows, columns, nodes,
              halo_turn):
    edges, width = found.shape
    unit = UNIT
    units = place.shape[0] // 8
    parts = width // LANES
    vmem = pl.BlockSpec(memory_space=pltpu.VMEM)
    smem = pl.BlockSpec(memory_space=pltpu.SMEM)
    hbm = pl.BlockSpec(memory_space=pltpu.HBM)
    return pl.pallas_call(
        functools.partial(edge_kernel, columns, halo_turn, rows),
        in_specs=[smem, hbm, hbm, vmem, vmem, vmem] + [vmem] * len(pieces),
        out_specs=vmem,
        out_shape=jax.ShapeDtypeStruct((nodes, width), jnp.float32),
        scratch_shapes=[
            pltpu.SMEM((units + 1,), jnp.int32),
            pltpu.SMEM((6, 8, LANES), jnp.int32),
            pltpu.VMEM((width, width), jnp.bfloat16),
            pltpu.VMEM((width, width), jnp.bfloat16),
            pltpu.VMEM((nodes * parts, LANES), jnp.float32),
            pltpu.VMEM((rows[3], width), jnp.bfloat16),
            pltpu.VMEM((unit * parts, LANES), jnp.float32),
            pltpu.VMEM((unit * parts, LANES), jnp.float32),
            pltpu.VMEM((6, unit, width), jnp.bfloat16),
            pltpu.VMEM((2 * unit, width), jnp.bfloat16),
            pltpu.SemaphoreType.DMA((6,)),
            pltpu.SemaphoreType.DMA((6,)),
        ],
        compiler_params=pltpu.CompilerParams(vmem_limit_bytes=40 << 20),
        cost_estimate=pl.CostEstimate(
            flops=edges * width * (width + 2 * nodes) // 2,
            bytes_accessed=edges * width // 2,
            transcendentals=edges * width // 4,
        ),
    )(bounds, found, place, recv, features, start, *pieces)


def swap_kernel(own_ref, far_ref, own_out, far_out, send, recv):
    beside = across(lax.axis_index("ch"), 1)
    barrier = pltpu.get_barrier_semaphore()
    pl.semaphore_signal(
        barrier, inc=1, device_id={"ch": beside}, device_id_type=pl.DeviceIdType.MESH
    )
    pl.semaphore_wait(barrier, 1)
    copies = [
        pltpu.make_async_remote_copy(
            src_ref=source, dst_ref=target, send_sem=send.at[n], recv_sem=recv.at[n],
            device_id={"ch": beside}, device_id_type=pl.DeviceIdType.MESH,
        )
        for n, (source, target) in enumerate(((own_ref, own_out), (far_ref, far_out)))
    ]
    for copy in copies:
        copy.start()
    for copy in copies:
        copy.wait()


def swapped_beside(own, far):
    vmem = pl.BlockSpec(memory_space=pltpu.VMEM)
    return pl.pallas_call(
        swap_kernel,
        in_specs=[vmem] * 2,
        out_specs=[vmem] * 2,
        out_shape=[jax.ShapeDtypeStruct(own.shape, own.dtype)] * 2,
        scratch_shapes=[pltpu.SemaphoreType.DMA((2,)), pltpu.SemaphoreType.DMA((2,))],
        compiler_params=pltpu.CompilerParams(
            vmem_limit_bytes=8 << 20, collective_id=0, has_side_effects=True
        ),
    )(own, far)


def across(me, bit):
    return me + bit - 2 * bit * lax.rem(me // bit, 2)


def swapped(block, bit, width):
    parts = block.shape[1] // width
    return jnp.concatenate(
        [block[:, (n ^ bit) * width:((n ^ bit) + 1) * width] for n in range(parts)], axis=1
    )


def tail_kernel(
    rows,
    totals_ref,
    recv_ref,
    message_bias_ref,
    *refs,
):
    ch_count = lax.axis_size("ch")
    pieces = refs[:ch_count]
    (out_ref, near, onward, far, normed, give, near_send, near_recv, far_send, far_recv,
     back_send, back_recv, messages) = refs[ch_count:]
    me = lax.axis_index("ch")
    parts, part, width = normed.shape
    beside, opposite = across(me, 1), across(me, 2)
    partners = [beside, opposite, across(opposite, 1)]
    barrier = pltpu.get_barrier_semaphore()
    for partner in partners:
        pl.semaphore_signal(
            barrier, inc=1, device_id={"ch": partner}, device_id_type=pl.DeviceIdType.MESH
        )
    pl.semaphore_wait(barrier, ch_count - 1)

    def copy_to(source, target, send, recv, partner):
        return pltpu.make_async_remote_copy(
            src_ref=source, dst_ref=target, send_sem=send, recv_sem=recv,
            device_id={"ch": partner}, device_id_type=pl.DeviceIdType.MESH,
        )

    nears = [
        copy_to(totals_ref.at[block], near.at[n], near_send.at[n], near_recv.at[n], beside)
        for n, block in enumerate((partners[2], beside))
    ]
    for copy in nears:
        copy.start()
    at = [sum(rows[:n]) for n in range(len(rows) + 1)]
    for n in range(parts):
        for j in range(parts):
            first = at[4] + j * width
            messages[n, :, j * width:(j + 1) * width] = pieces[n][first:first + width, :]
    nears[0].wait()
    onward[...] = (totals_ref[opposite] + swapped(near[0], 1, width)).astype(onward.dtype)
    pass_on = copy_to(onward, far, far_send.at[0], far_recv.at[0], opposite)
    pass_on.start()

    def tally(n, counts):
        nodes_here = lax.broadcasted_iota(jnp.int32, (part, LANES), 0) + me * part
        for i in range(8):
            ids = recv_ref[pl.ds(n * 8 + i, 1), :]
            counts = counts + jnp.where(nodes_here == ids, 1.0, 0.0)
        return counts

    counts = lax.fori_loop(
        0, recv_ref.shape[0] // 8, tally, jnp.zeros((part, LANES), jnp.float32)
    )
    aggregated = jnp.sum(counts, axis=1, keepdims=True) * message_bias_ref[...]
    nears[1].wait()
    sums = totals_ref[me] + swapped(near[1], 1, width)
    pass_on.wait()
    sums = sums + swapped(far[...].astype(jnp.float32), 2, width)
    for n in range(parts):
        rest = sums[:, n * width:(n + 1) * width]
        for _ in range(2):
            piece = rest.astype(jnp.bfloat16)
            aggregated += jnp.dot(
                piece, messages[n], preferred_element_type=jnp.float32
            )
            rest = rest - piece.astype(jnp.float32)
    centre = jnp.mean(aggregated, axis=1, keepdims=True)
    spread = jnp.mean(jnp.square(aggregated - centre), axis=1, keepdims=True)
    result = (aggregated - centre) * lax.rsqrt(spread + 1.0)
    for n in range(parts):
        normed[n] = result[:, n * width:(n + 1) * width]
    mine = pl.ds(pl.multiple_of(me * part, part), part)
    returns = []
    for j in (3, 2, 1, 0):
        owner = ([me] + partners)[j]
        small = pieces[j][at[3]:at[4], :].astype(jnp.float32)
        gain = small[7:8] + small[8:9] + small[9:10]
        shift = small[10:11] + small[11:12] + small[12:13]
        latent = pieces[j][pl.ds(at[2] + pl.multiple_of(me * part, part), part), :]
        block = (latent.astype(jnp.float32) + normed[owner] * gain + shift).astype(out_ref.dtype)
        if j == 0:
            out_ref[mine, :] = block
            continue
        give[j - 1] = block
        copy = copy_to(
            give.at[j - 1], out_ref.at[mine, :], back_send.at[j - 1], back_recv.at[j - 1], owner
        )
        copy.start()
        returns.append(copy)
    for copy in returns:
        copy.wait()


def finished(totals, recv, message_bias, pieces, rows, nodes):
    ch_count = lax.axis_size("ch")
    part = nodes // ch_count
    full = totals.shape[1]
    width = full // ch_count
    vmem = pl.BlockSpec(memory_space=pltpu.VMEM)
    return pl.pallas_call(
        functools.partial(tail_kernel, rows),
        in_specs=[vmem] * (3 + ch_count),
        out_specs=vmem,
        out_shape=jax.ShapeDtypeStruct((nodes, width), jnp.bfloat16),
        scratch_shapes=[
            pltpu.VMEM((2, part, full), jnp.float32),
            pltpu.VMEM((part, full), jnp.bfloat16),
            pltpu.VMEM((part, full), jnp.bfloat16),
            pltpu.VMEM((ch_count, part, width), jnp.float32),
            pltpu.VMEM((ch_count - 1, part, width), jnp.bfloat16),
            pltpu.SemaphoreType.DMA((2,)),
            pltpu.SemaphoreType.DMA((2,)),
            pltpu.SemaphoreType.DMA((1,)),
            pltpu.SemaphoreType.DMA((1,)),
            pltpu.SemaphoreType.DMA((ch_count - 1,)),
            pltpu.SemaphoreType.DMA((ch_count - 1,)),
            pltpu.VMEM((ch_count, width, full), jnp.bfloat16),
        ],
        compiler_params=pltpu.CompilerParams(
            vmem_limit_bytes=32 << 20, collective_id=1, has_side_effects=True
        ),
    )(totals.reshape(ch_count, part, full), recv, message_bias.reshape(1, -1), *pieces)


def on_device(
    grid_inputs,
    embed_weight,
    embed_bias,
    mesh_latent,
    edge_features,
    senders,
    receivers,
    sender_weight,
    receiver_weight,
    feature_weight,
    hidden_bias,
    message_weight,
    message_bias,
    norm_gain,
    norm_shift,
):
    lon_count, ch_count = lax.axis_size("lon"), lax.axis_size("ch")
    assert ch_count == 4
    columns = grid_inputs.shape[0] // LAT
    assert columns >= WINDOW
    mesh_nodes = mesh_latent.shape[0]
    width = embed_weight.shape[1]
    assert width == PARTS * LANES
    edges = senders.shape[0]
    unit = UNIT
    assert edges % unit == 0 and unit == 2 * CHUNK
    points = grid_inputs.T

    edge_columns, packed, send, recv, place, bounds = prepared(
        points, senders, receivers, sender_weight, receiver_weight, mesh_latent,
        feature_weight, hidden_bias, norm_gain, norm_shift, message_weight,
    )
    rows = (width, width, mesh_nodes, 16)
    hops = []
    for i in range(lon_count):
        hops.append((i * ch_count, (i + 1) % lon_count * ch_count))
        hops.append(
            (i * ch_count + ch_count - 1, (i - 1) % lon_count * ch_count + ch_count - 1)
        )
    halo = lax.ppermute(edge_columns, ("lon", "ch"), hops)

    opposite = lax.ppermute(packed, "ch", [(i, i ^ 2) for i in range(ch_count)])
    beside, diagonal = swapped_beside(packed, opposite)
    pieces = [packed, beside, opposite, diagonal]

    totals = jnp.zeros((8, LANES), jnp.float32)
    for halo_turn in (False, True):
        found = gathered(
            bounds, send, points, halo if halo_turn else None, embed_weight, embed_bias,
            halo_turn,
        )
        totals = node_sums(
            bounds, found, place, recv, edge_features, totals, pieces, rows, columns, mesh_nodes, halo_turn,
        )
    return finished(
        totals, recv, message_bias, pieces, rows, mesh_nodes
    )


def solution(mesh):
    return jax.shard_map(
        on_device,
        mesh=mesh,
        in_specs=(
            P("lon", None),
            P(),
            P(),
            P("lon", "ch"),
            P(None, "lon"),
            P("lon"),
            P("lon"),
            P(None, "ch"),
            P(None, "ch"),
            P(None, "ch"),
            P("ch"),
            P("ch", None),
            P(),
            P("ch"),
            P("ch"),
        ),
        out_specs=P("lon", "ch"),
        check_vma=False,
    )
```

time: 95.7 us -> 69.4 us (0.73); the launches traced: 94 us -> 69.1 us
  local copies, waits for them, and re-layouts: 14.1 us -> 2.28 us
  starting transfers between devices: 14.1 us -> 4.95 us
  other arithmetic: 4.97 us -> 0 us
  waiting for transfers between devices: 0.02 us -> 1.2 us
    ppermute x6 -> x1, starting transfers between devices: 10.5 us -> 0.07 us  [on_device(): opposite = lax.ppermute(packed, 'ch', [(i, i ^ 2) for i in range(ch_count)])]
    pallas_call x0 -> x2, Pallas kernels: none -> 9.75 us  [the longest x1 5.11 us: swapped_beside(): pl.pallas_call(swap_kernel, in_specs=[vmem] * 2, out_specs=[vmem] * 2, ou...]
    pallas_call x1, Pallas kernels: 16.6 us -> 11.4 us  [finished(): pl.pallas_call(functools.partial(tail_kernel, rows), in_specs=[vmem] * (3...]
    concatenate x3 -> x0, local copies, waits for them, and re-layouts: 3.69 us -> none  [the longest x1 3.53 us: on_device(): pieces = swap(jnp.concatenate(blocks))]
    dynamic_slice x1 -> x0, local copies, waits for them, and re-layouts: 3.42 us -> none  [on_device(): lax.dynamic_slice(points, (0, edge_start), (points.shape[0], HALO * LAT))]
    reshape x3 -> x0, local copies, waits for them, and re-layouts: 3.36 us -> none  [the longest x1 1.54 us: on_device(): (recv * parts).reshape(-1, unit)]
    pallas_call x2, Pallas kernels: 22.8 us -> 19.9 us  [gathered(): pl.pallas_call(functools.partial(gather_kernel, columns, halo_turn), in_s...]
    concatenate x1 -> x0, other arithmetic: 1.97 us -> none  [on_device(): jnp.concatenate([edge_features, jnp.ones((3, edges), jnp.bfloat16), jnp.z...]
  transfers between devices with their start and end apart: 7 -> 2, of which waited for: 0 -> 1; matrix products, arithmetic and copies ran while one was open for 11% -> 0% of each run, Pallas kernels for 47% -> 41%
where the time goes in v2:
time: 69.4 us; the launch traced here: 69.1 us
  Pallas kernels  60.6 us (87%)
  starting transfers between devices  4.95 us (7%)
  local copies, waits for them, and re-layouts  2.28 us (3%)
  waiting for transfers between devices  1.2 us (2%)
    pallas_call x2, Pallas kernels, gathered(): pl.pallas_call(functools.partial(gather_kernel, columns, halo_turn), in_s...  19.9 us
    pallas_call x2, Pallas kernels, node_sums(): pl.pallas_call(functools.partial(edge_kernel, columns, halo_turn, rows),...  19.5 us
    pallas_call x1, Pallas kernels, finished(): pl.pallas_call(functools.partial(tail_kernel, rows), in_specs=[vmem] * (3...  11.4 us
    pallas_call x1, Pallas kernels, swapped_beside(): pl.pallas_call(swap_kernel, in_specs=[vmem] * 2, out_specs=[vmem] * 2, ou...  5.11 us
    ppermute x1, starting transfers between devices, on_device(): halo = lax.ppermute(edge_columns, ('lon', 'ch'), hops)  4.87 us
    pallas_call x1, Pallas kernels, prepared(): pl.pallas_call(functools.partial(prepare_kernel, columns), in_specs=[hbm]...  4.64 us
    unnamed x19, local copies, waits for them, and re-layouts  2.28 us
  transfers between devices with their start and end apart: 2, of which 1 were waited for; matrix products, arithmetic and copies ran while one was open for 0% of the time, Pallas kernels for 41%

profile of v2, /device:TPU:0, one launch (start us, length us, event | category | flops | bytes accessed | tf_op | source)
XLA Modules:
  0.0 69.1 jit_solution(13580596897712767175)
XLA Ops:
  0.0 0.0 copy-start.1
  0.0 0.0 copy-start.4
  0.0 4.6 %shard_map.145 = (bf16[474,2560]{1,0:T(8,128)(2,1)}, bf16[2192,128]{1,0:T(8,128)(2,1)}, s32[352,128]{1,0:T(8,128)}, s32[176,128]{1,0:T(8,128)}, s32[352,128]{1,0:T(8,128)}, /*index=5*/s32[2,256]{1,0:T(2,128)}) custom-call(bf16[474,28800]{1,0:T(8,128)(2,1)} %bitcast.13, s32[176,128]{1,0:T(8,128)} %bitcast.17, s32[176,128]{1,0:T(8,128)} %bitcast.18, ...), custom_call_target="tpu_custom_call" | custom-call | tf_op jit(solution)/shard_map/pallas_call | solution.py:184
  4.7 4.9 %collective-permute-start = (bf16[474,2560]{1,0:T(8,128)(2,1)}, bf16[474,2560]{1,0:T(8,128)(2,1)S(1)}, u32[]{:S(2)}, u32[]{:S(2)}) collective-permute-start(bf16[474,2560]{1,0:T(8,128)(2,1)} %get-tuple-element.15), channel_id=1, source_target_pairs={{0,4},{3,31},{4,8},{7,3},{8,12},{11,7},{12,16},{15,11},{16,20},{19... | collective-permute-start | bytes 7280648 | tf_op jit(solution)/shard_map/ppermute | solution.py:809
  9.5 0.1 collective-permute-start.1
  9.6 0.0 copy-done.1
  9.6 0.0 copy-done.4
  9.6 0.0 copy-start.2
  9.6 0.9 %copy-done.2 = s32[352,128]{1,0:T(8,128)S(1)} copy-done((s32[352,128]{1,0:T(8,128)S(1)}, s32[352,128]{1,0:T(8,128)}, u32[]{:S(2)}) %copy-start.2) | copy-done | bytes 180248
  10.6 0.0 copy-start.5
  10.6 0.7 copy-done.5
  11.2 0.0 copy-start
  11.2 0.0 copy-start.3
  11.2 0.0 copy-start.7
  11.2 0.0 copy-start.8
  11.2 11.6 %shard_map.147.gathered_ref = bf16[22784,512]{1,0:T(8,128)(2,1)} custom-call(s32[2,256]{1,0:T(2,128)S(1)} %copy-done.5, s32[352,128]{1,0:T(8,128)S(1)} %copy-done.2, bf16[474,28800]{1,0:T(8,128)(2,1)} %bitcast.14, bf16[474,28800]{1,0:T(8,128)(2,1)} %bitcast.15, bf16[474,512]{1,0:T(8,128)(2,1)S(1)} %copy-done.1, f32[1,512]{1,0:T(1,128)S(1)} %bitcast.10), custom_call_target="tpu_custom_call" | custom-call | flops 10934550528 | bytes 11534336 | tf_op jit(solution)/shard_map/pallas_call | solution.py:386
  22.8 1.2 %collective-permute-done.1.far_ref.refs_2_ = bf16[2192,128]{1,0:T(8,128)(2,1)S(1)} collective-permute-done((bf16[2192,128]{1,0:T(8,128)(2,1)}, bf16[2192,128]{1,0:T(8,128)(2,1)S(1)}, u32[]{:S(2)}, u32[]{:S(2)}) %collective-permute-start.1) | collective-permute-done | bytes 561184 | tf_op jit(solution)/shard_map/ppermute | solution.py:811
  24.0 0.0 copy-done
  24.0 5.1 %shard_map.148 = (bf16[2192,128]{1,0:T(8,128)(2,1)S(1)}, bf16[2192,128]{1,0:T(8,128)(2,1)S(1)}) custom-call(bf16[2192,128]{1,0:T(8,128)(2,1)S(1)} %copy-done, bf16[2192,128]{1,0:T(8,128)(2,1)S(1)} %collective-permute-done.1.far_ref.refs_2_), custom_call_target="tpu_custom_call" | custom-call | tf_op jit(solution)/shard_map/pallas_call | solution.py:621
  29.1 0.0 copy-done.3
  29.1 0.0 copy-done.7
  29.1 0.0 copy-done.8
  29.2 11.6 %shard_map.149.start_ref = f32[640,512]{1,0:T(8,128)S(1)} custom-call(s32[2,256]{1,0:T(2,128)S(1)} %copy-done.5, bf16[22784,512]{1,0:T(8,128)(2,1)} %shard_map.147.gathered_ref, s32[352,128]{1,0:T(8,128)S(1)} %copy-done.8, s32[176,128]{1,0:T(8,128)S(1)} %copy-done.3, bf16[4,22528]{1,0:T(4,128)(2,1)S(1)} %copy-done.7, ...), custom_call_target="tpu_custom_call" | custom-call | flops 10452205568 | bytes 5832704 | tf_op jit(solution)/shard_map/pallas_call | solution.py:571
  40.7 0.0 collective-permute-done.halo_ref
  40.7 8.3 %shard_map.146.gathered_ref = bf16[22784,512]{1,0:T(8,128)(2,1)} custom-call(s32[2,256]{1,0:T(2,128)S(1)} %copy-done.5, s32[352,128]{1,0:T(8,128)S(1)} %copy-done.2, bf16[474,28800]{1,0:T(8,128)(2,1)} %bitcast.16, bf16[474,2560]{1,0:T(8,128)(2,1)S(1)} %collective-permute-done.halo_ref, bf16[474,512]{1,0:T(8,128)(2,1)S(1)} %copy-done.1, f32[1,512]{1,0:T(1,128)S(1)} %bitcast.11), custom_call_target="tpu_custom_call" | custom-call | flops 10934550528 | bytes 11534336 | tf_op jit(solution)/shard_map/pallas_call | solution.py:386
  49.1 0.0 copy-start.6
  49.1 7.9 %shard_map.150 = f32[640,512]{1,0:T(8,128)S(1)} custom-call(s32[2,256]{1,0:T(2,128)S(1)} %copy-done.5, bf16[22784,512]{1,0:T(8,128)(2,1)} %shard_map.146.gathered_ref, s32[352,128]{1,0:T(8,128)S(1)} %copy-done.8, s32[176,128]{1,0:T(8,128)S(1)} %copy-done.3, bf16[4,22528]{1,0:T(4,128)(2,1)S(1)} %copy-done.7, f32[640,512]{1,0:T(8,128)S(1)} %shard_map.149.start_ref, ...), custom_call_target="tpu_custom_call" | custom-call | flops 10452205568 | bytes 5832704 | tf_op jit(solution)/shard_map/pallas_call | solution.py:571
  57.0 0.0 copy-done.6
  57.0 11.4 %shard_map.151 = bf16[640,128]{1,0:T(8,128)(2,1)S(1)} custom-call(f32[4,160,512]{2,1,0:T(8,128)S(1)} %bitcast.9, s32[176,128]{1,0:T(8,128)S(1)} %copy-done.3, f32[1,512]{1,0:T(1,128)S(1)} %bitcast.12, bf16[2192,128]{1,0:T(8,128)(2,1)S(1)} %copy-done, bf16[2192,128]{1,0:T(8,128)(2,1)S(1)} %get-tuple-element.19.refs_1_, ...), custom_call_target="tpu_custom_call" | custom-call | tf_op jit(solution)/shard_map/pallas_call | solution.py:744
  68.5 0.7 copy.17
  (1 shorter events, 0.0 us)
Async XLA Ops:
  0.0 9.6 %copy-start.1 = (bf16[474,512]{1,0:T(8,128)(2,1)S(1)}, bf16[474,512]{1,0:T(8,128)(2,1)}, u32[]{:S(2)}) copy-start(bf16[474,512]{1,0:T(8,128)(2,1)} %embed_ref.3) | copy-start | bytes 1456132
  0.0 9.6 %copy-start.4 = (f32[512]{0:T(512)S(1)}, f32[512]{0:T(512)}, u32[]{:S(2)}) copy-start(f32[512]{0:T(512)} %param.17) | copy-start | bytes 6148
  4.7 36.1 %collective-permute-start = (bf16[474,2560]{1,0:T(8,128)(2,1)}, bf16[474,2560]{1,0:T(8,128)(2,1)S(1)}, u32[]{:S(2)}, u32[]{:S(2)}) collective-permute-start(bf16[474,2560]{1,0:T(8,128)(2,1)} %get-tuple-element.15), channel_id=1, source_target_pairs={{0,4},{3,31},{4,8},{7,3},{8,12},{11,7},{12,16},{15,11},{16,20},{19... | collective-permute-start | bytes 7280648 | tf_op jit(solution)/shard_map/ppermute | solution.py:809
  9.5 14.5 %collective-permute-start.1 = (bf16[2192,128]{1,0:T(8,128)(2,1)}, bf16[2192,128]{1,0:T(8,128)(2,1)S(1)}, u32[]{:S(2)}, u32[]{:S(2)}) collective-permute-start(bf16[2192,128]{1,0:T(8,128)(2,1)} %get-tuple-element.18.own_ref.refs_0_), channel_id=1, source_target_pairs={{0,2},{1,3},{2,0},{3,1},{4,6},{5,7},{6,4},{7,5},{8,10},{9,11},{10,... | collective-permute-start | bytes 1683464 | tf_op jit(solution)/shard_map/ppermute | solution.py:811
  9.6 0.9 %copy-start.2 = (s32[352,128]{1,0:T(8,128)S(1)}, s32[352,128]{1,0:T(8,128)}, u32[]{:S(2)}) copy-start(s32[352,128]{1,0:T(8,128)} %get-tuple-element.14.send_ref) | copy-start | bytes 540676
  10.6 0.7 copy-start.5
  11.2 12.8 %copy-start = (bf16[2192,128]{1,0:T(8,128)(2,1)S(1)}, bf16[2192,128]{1,0:T(8,128)(2,1)}, u32[]{:S(2)}) copy-start(bf16[2192,128]{1,0:T(8,128)(2,1)} %get-tuple-element.18.own_ref.refs_0_) | copy-start | bytes 1683460
  11.2 17.9 %copy-start.3 = (s32[176,128]{1,0:T(8,128)S(1)}, s32[176,128]{1,0:T(8,128)}, u32[]{:S(2)}) copy-start(s32[176,128]{1,0:T(8,128)} %get-tuple-element.17.recv_ref) | copy-start | bytes 270340
  11.2 17.9 %copy-start.7 = (bf16[4,22528]{1,0:T(4,128)(2,1)S(1)}, bf16[4,22528]{1,0:T(4,128)(2,1)}, u32[]{:S(2)}) copy-start(bf16[4,22528]{1,0:T(4,128)(2,1)} %features_ref.3) | copy-start | bytes 540676
  11.2 17.9 %copy-start.8 = (s32[352,128]{1,0:T(8,128)S(1)}, s32[352,128]{1,0:T(8,128)}, u32[]{:S(2)}) copy-start(s32[352,128]{1,0:T(8,128)} %get-tuple-element.16.place_ref) | copy-start | bytes 540676
  49.1 8.0 %copy-start.6 = (f32[512]{0:T(512)S(1)}, f32[512]{0:T(512)}, u32[]{:S(2)}) copy-start(f32[512]{0:T(512)} %param.27) | copy-start | bytes 6148

commit v3 on v2

--- a/solution.py
+++ b/solution.py
@@ -20,6 +20,10 @@
 
 def silu_of_double(half):
     return half + half * jnp.tanh(half)
+
+
+def turn_units(units, ch_count):
+    return -(-units * 5 // (8 * ch_count))
 
 
 def low_of(bounds_ref, u):
@@ -44,7 +48,7 @@
     middle = lambda k: first + lax.div((last - first) * (k - 1), ch_count - 2)
     begin = jnp.where(me == 0, 0, middle(me))
     end = jnp.where(me == ch_count - 1, inner_count, middle(me + 1))
-    first_turn = -(-units * 5 // (8 * ch_count))
+    first_turn = turn_units(units, ch_count)
     count, rank = jnp.int32(0), jnp.int32(0)
     for u in range(units):
         inner = 1 - at_left[u] - at_right[u]
@@ -119,6 +123,9 @@
     ]
     for copy in takes + loads:
         copy.start()
+    for take, give in zip(takes, gives):
+        take.wait()
+        give.start()
     for copy in loads:
         copy.wait()
     singles = [feature_ref[...].astype(jnp.float32)]
@@ -159,9 +166,6 @@
             [best, jnp.full((tall - best.shape[0], LANES), fill, jnp.int32)]
         )
         bounds_ref[n:n + 1, :] = pick(jnp.transpose(best), axis=0, keepdims=True)
-    for take, give in zip(takes, gives):
-        take.wait()
-        give.start()
     for give in gives:
         give.wait()
     pack.wait()
@@ -217,40 +221,46 @@
     return pl.ds(pl.multiple_of(u * 8, 8), 8)
 
 
-def gather_kernel(
-    columns,
-    halo_turn,
-    bounds_ref,
-    send_ref,
-    x_ref,
-    halo_ref,
-    embed_ref,
-    bias_ref,
-    out_ref,
-    list_ref,
-    events,
-    event_at,
-    held_column,
-    index_even,
-    index_odd,
-    points,
-    table,
-    even,
-    odd,
-    packed,
-    embed_half,
-    index_sem,
-    point_sem,
-    out_sem,
-):
+def point_scratch(units, channels, width):
+    parts = width // LANES
+    return [
+        pltpu.SMEM((units + 1,), jnp.int32),
+        pltpu.SMEM((units * WINDOW + 1,), jnp.int32),
+        pltpu.SMEM((units + 1,), jnp.int32),
+        pltpu.SMEM((SLOTS,), jnp.int32),
+        pltpu.SMEM((8, LANES), jnp.int32),
+        pltpu.SMEM((8, LANES), jnp.int32),
+        pltpu.VMEM((6, channels, LAT), jnp.bfloat16),
+        pltpu.VMEM((SLOTS * LAT * parts, LANES), jnp.float32),
+        pltpu.VMEM((CHUNK * parts, LANES), jnp.float32),
+        pltpu.VMEM((CHUNK * parts, LANES), jnp.float32),
+        pltpu.VMEM((channels, width), jnp.bfloat16),
+        pltpu.VMEM((1, width), jnp.float32),
+        pltpu.SemaphoreType.DMA((2,)),
+        pltpu.SemaphoreType.DMA((6,)),
+        pltpu.SemaphoreType.DMA((2,)),
+    ]
+
+
+POINT_SCRATCH = 15
+
+
+def point_tools(columns, later, bounds_ref, send_ref, x_ref, halo_ref, embed_ref, bias_ref,
+                scratch):
+    (list_ref, events, event_at, held_column, index_even, index_odd, points, table, even, odd,
+     embed_half, bias_half, index_sem, point_sem, weight_sem) = scratch
     index = (index_even, index_odd)
-    parts = out_ref.shape[1] // LANES
-    unit = UNIT
+    parts = embed_half.shape[1] // LANES
     step = LAT * parts
     depth = points.shape[0]
-    count = pick_units(bounds_ref, list_ref, list_ref.shape[0] - 1, columns, halo_turn)
-
-    embed_half[...] = embed_ref[...] * jnp.bfloat16(0.5)
+    weights = [
+        pltpu.make_async_copy(source, target, weight_sem.at[n])
+        for n, (source, target) in enumerate(((embed_ref, embed_half), (bias_ref, bias_half)))
+    ]
+    for copy in weights:
+        copy.start()
+    count = pick_units(bounds_ref, list_ref, list_ref.shape[0] - 1, columns, later)
+
     for n in range(SLOTS):
         held_column[n] = -1
 
@@ -265,9 +275,7 @@
             events[total] = column
             return total + new
 
-        return lax.fori_loop(
-            low_of(bounds_ref, u), high_of(bounds_ref, u) + 1, note, total
-        )
+        return lax.fori_loop(low_of(bounds_ref, u), high_of(bounds_ref, u) + 1, note, total)
 
     total = lax.fori_loop(0, count, note_unit, jnp.int32(0))
     event_at[count] = total
@@ -281,7 +289,7 @@
                 source.at[:, pl.ds(start, LAT)], points.at[slot], point_sem.at[slot]
             )
 
-        if not halo_turn:
+        if not later:
             copy(x_ref, column - HALO).start()
             return
         last = column >= HALO + columns
@@ -291,15 +299,22 @@
         )
         pl.when(jnp.logical_not(outside))(lambda: copy(x_ref, column - HALO).start())
 
-    def fetch_index(n, slot):
+    def index_copy(n, turn):
         return pltpu.make_async_copy(
-            send_ref.at[index_rows(list_ref[n]), :], index[slot], index_sem.at[slot]
-        )
-
-    for event in range(depth):
-        pl.when(event < total)(functools.partial(fetch, event))
+            send_ref.at[index_rows(list_ref[n]), :], index[turn], index_sem.at[turn]
+        )
+
+    def fetch_first(event, carry):
+        fetch(event)
+        return carry
+
+    lax.fori_loop(0, jnp.minimum(total, depth), fetch_first, 0)
     for n in range(2):
-        pl.when(n < count)(lambda n=n: fetch_index(n, n).start())
+        pl.when(n < count)(lambda n=n: index_copy(n, n).start())
+    for copy in weights:
+        copy.wait()
+    embed_half[...] = embed_half[...] * jnp.bfloat16(0.5)
+    bias_half[...] = bias_half[...] * 0.5
 
     def one_event(event, carry):
         slot = lax.rem(event, depth)
@@ -309,7 +324,7 @@
         before = lax.dot_general(
             points[slot], embed_half[...], (((0,), (0,)), ((), ())),
             preferred_element_type=jnp.float32,
-        ) + 0.5 * bias_ref[...]
+        ) + bias_half[...]
         latent = silu_of_double(before)
         base = lax.rem(events[event], SLOTS) * step
         for j in range(parts):
@@ -317,44 +332,47 @@
         pl.when(event + depth < total)(lambda: fetch(event + depth))
         return carry
 
-    def gather(slot, half, held):
+    def bring(n, turn):
+        lax.fori_loop(event_at[n], event_at[n + 1], one_event, 0)
+        index_copy(n, turn).wait()
+
+    def gather(turn, half):
+        held = (even, odd)[half]
         row = half * (CHUNK // LANES)
         for i in range(CHUNK):
-            place = pl.multiple_of(index[slot][row + i // LANES, i % LANES], parts)
+            place = pl.multiple_of(index[turn][row + i // LANES, i % LANES], parts)
             held[pl.ds(parts * i, parts), :] = table[pl.ds(place, parts), :]
 
-    def leave(start, slot, held):
+    def leave(half, target, start):
+        held = (even, odd)[half]
         for j in range(parts):
-            packed[slot, :, j * LANES:(j + 1) * LANES] = (
+            target[pl.ds(start, CHUNK), j * LANES:(j + 1) * LANES] = (
                 held[pl.ds(j, CHUNK, stride=parts), :].astype(jnp.bfloat16)
             )
-        pltpu.make_async_copy(
-            packed.at[slot],
-            out_ref.at[pl.ds(pl.multiple_of(start, CHUNK), CHUNK), :],
-            out_sem.at[slot],
-        ).start()
-
-    def settle(slot):
-        pltpu.make_async_copy(
-            packed.at[slot], out_ref.at[pl.ds(0, CHUNK), :], out_sem.at[slot]
-        ).wait()
-
+
+    def next_index(n, turn):
+        pl.when(n + 2 < count)(lambda: index_copy(n + 2, turn).start())
+
+    return count, list_ref, bring, gather, leave, next_index
+
+
+def gather_kernel(columns, bounds_ref, send_ref, x_ref, embed_ref, bias_ref, out_ref, *scratch):
+    count, _, bring, gather, leave, next_index = point_tools(
+        columns, False, bounds_ref, send_ref, x_ref, None, embed_ref, bias_ref, scratch
+    )
     spare = out_ref.shape[0] - CHUNK
 
     def second_half(n):
-        earlier = list_ref[jnp.maximum(n - 1, 0)] * unit + CHUNK
-        return jnp.where(n > 0, earlier, spare)
+        place = jnp.where(n > 0, (n - 1) * UNIT + CHUNK, spare)
+        return pl.multiple_of(place, CHUNK)
 
     def one_unit(n, turn):
-        lax.fori_loop(event_at[n], event_at[n + 1], one_event, 0)
-        fetch_index(n, turn).wait()
-        for slot in (turn, 2 + turn):
-            pl.when(n > 1)(functools.partial(settle, slot))
-        leave(second_half(n), 2 + turn, odd)
-        gather(turn, 0, even)
-        leave(list_ref[n] * unit, turn, even)
-        gather(turn, 1, odd)
-        pl.when(n + 2 < count)(lambda: fetch_index(n + 2, turn).start())
+        bring(n, turn)
+        leave(1, out_ref, second_half(n))
+        gather(turn, 0)
+        leave(0, out_ref, pl.multiple_of(n * UNIT, UNIT))
+        gather(turn, 1)
+        next_index(n, turn)
 
     def two_units(m, carry):
         one_unit(2 * m, 0)
@@ -362,89 +380,90 @@
         return carry
 
     lax.fori_loop(0, (count + 1) // 2, two_units, 0)
-
-    @pl.when(count > 0)
-    def _():
-        turn = lax.rem(count, 2)
-        for slot in (turn, 2 + turn):
-            pl.when(count > 1)(functools.partial(settle, slot))
-        leave(second_half(count), 2 + turn, odd)
-        settle(2 + turn)
-        for slot in (1 - turn, 3 - turn):
-            settle(slot)
-
-
-def gathered(bounds, send, points, halo, embed_weight, embed_bias, halo_turn):
+    pl.when(count > 0)(lambda: leave(1, out_ref, second_half(count)))
+
+
+def gathered(bounds, send, points, embed_weight, embed_bias):
     channels, width = embed_weight.shape
     columns = points.shape[1] // LAT
-    parts = width // LANES
-    unit = UNIT
     units = send.shape[0] // 8
+    most = turn_units(units, lax.axis_size("ch"))
     vmem = pl.BlockSpec(memory_space=pltpu.VMEM)
     smem = pl.BlockSpec(memory_space=pltpu.SMEM)
     hbm = pl.BlockSpec(memory_space=pltpu.HBM)
     return pl.pallas_call(
-        functools.partial(gather_kernel, columns, halo_turn),
-        in_specs=[smem, hbm, hbm, hbm, vmem, vmem],
-        out_specs=hbm,
-        out_shape=jax.ShapeDtypeStruct((units * unit + CHUNK, width), jnp.bfloat16),
-        scratch_shapes=[
-            pltpu.SMEM((units + 1,), jnp.int32),
-            pltpu.SMEM((units * WINDOW + 1,), jnp.int32),
-            pltpu.SMEM((units + 1,), jnp.int32),
-            pltpu.SMEM((SLOTS,), jnp.int32),
-            pltpu.SMEM((8, LANES), jnp.int32),
-            pltpu.SMEM((8, LANES), jnp.int32),
-            pltpu.VMEM((6, channels, LAT), jnp.bfloat16),
-            pltpu.VMEM((SLOTS * LAT * parts, LANES), jnp.float32),
-            pltpu.VMEM((CHUNK * parts, LANES), jnp.float32),
-            pltpu.VMEM((CHUNK * parts, LANES), jnp.float32),
-            pltpu.VMEM((4, CHUNK, width), jnp.bfloat16),
-            pltpu.VMEM((channels, width), jnp.bfloat16),
-            pltpu.SemaphoreType.DMA((2,)),
-            pltpu.SemaphoreType.DMA((6,)),
-            pltpu.SemaphoreType.DMA((4,)),
-        ],
+        functools.partial(gather_kernel, columns),
+        in_specs=[smem, hbm, hbm, hbm, hbm],
+        out_specs=vmem,
+        out_shape=jax.ShapeDtypeStruct((most * UNIT + CHUNK, width), jnp.bfloat16),
+        scratch_shapes=point_scratch(units, channels, width),
         compiler_params=pltpu.CompilerParams(vmem_limit_bytes=40 << 20),
         cost_estimate=pl.CostEstimate(
-            flops=2 * units * unit * channels * width,
-            bytes_accessed=units * unit * width,
-            transcendentals=units * unit * width // 2,
+            flops=2 * units * UNIT * channels * width,
+            bytes_accessed=units * UNIT * width,
+            transcendentals=units * UNIT * width // 2,
         ),
-    )(bounds, send, points, points if halo is None else halo,
-      embed_weight, embed_bias.reshape(1, -1))
+    )(bounds, send, points, embed_weight, embed_bias.reshape(1, -1))
+
+
+def sum_tools(list_ref, features_ref, recv_ref, sender_all, feature_all, hidden, out_ref):
+    nodes, width = out_ref.shape
+    parts = width // LANES
+    components = features_ref.shape[0]
+
+    def activate(n, turn, rows, terms):
+        start = pl.multiple_of(list_ref[n] * UNIT, UNIT)
+        mine = slice(turn * UNIT, (turn + 1) * UNIT)
+        before = jnp.dot(rows, sender_all[...], preferred_element_type=jnp.float32)
+        before += lax.dot_general(
+            features_ref[:, pl.ds(start, UNIT)], feature_all[:components, :],
+            (((0,), (0,)), ((), ())),
+            preferred_element_type=jnp.float32,
+        )
+        for j in range(parts):
+            lanes = slice(j * LANES, (j + 1) * LANES)
+            hidden[mine, lanes] = silu_of_double(
+                before[:, lanes] + terms[pl.ds(j, UNIT, stride=parts), :]
+            ).astype(jnp.bfloat16)
+
+    def add_up(first, turn, number, live=True):
+        each = lax.broadcasted_iota(jnp.int32, (nodes, LANES), 0)
+        blocks = []
+        for n in range(number):
+            for b in range(UNIT // LANES):
+                ids = recv_ref[pl.ds(list_ref[first + n] * (UNIT // LANES) + b, 1), :]
+                ids = ids if live is True else jnp.where(live, ids, -1)
+                blocks.append(jnp.where(each == ids, 1.0, 0.0))
+        by_node = jnp.concatenate(blocks, axis=1).astype(jnp.bfloat16)
+        mine = slice(turn * UNIT, (turn + number) * UNIT)
+        out_ref[...] += jnp.dot(by_node, hidden[mine, :], preferred_element_type=jnp.float32)
+
+    return activate, add_up
 
 
 def edge_kernel(
     columns,
-    halo_turn,
     rows,
     bounds_ref,
-    gathered_ref,
+    found_ref,
     place_ref,
     recv_ref,
     features_ref,
-    start_ref,
     *refs,
 ):
     ways = lax.axis_size("ch")
     pieces = refs[:ways]
-    (out_ref, list_ref, index, sender_all, receiver_all, recv_terms, feature_all, even, odd,
-     held, hidden, index_sem, sem) = refs[ways:]
+    (out_ref, sender_all, recv_terms, feature_all, list_ref, index, receiver_all, even, odd,
+     hidden, index_sem) = refs[ways:]
     me = lax.axis_index("ch")
     nodes, width = out_ref.shape
     part = width // ways
     parts = width // LANES
-    unit = UNIT
     rings = index.shape[0]
-    count = pick_units(bounds_ref, list_ref, list_ref.shape[0] - 1, columns, halo_turn)
-
-    def fetch(n):
-        slot = lax.rem(n, rings)
-        start = pl.multiple_of(list_ref[n] * unit, unit)
-        return pltpu.make_async_copy(
-            gathered_ref.at[pl.ds(start, unit), :], held.at[slot], sem.at[slot]
-        )
+    count = pick_units(bounds_ref, list_ref, list_ref.shape[0] - 1, columns, False)
+    activate, add_up = sum_tools(
+        list_ref, features_ref, recv_ref, sender_all, feature_all, hidden, out_ref
+    )
 
     def fetch_index(n):
         slot = lax.rem(n, rings)
@@ -452,12 +471,8 @@
             place_ref.at[index_rows(list_ref[n]), :], index.at[slot], index_sem.at[slot]
         )
 
-    def fetch_both(n):
-        fetch_index(n).start()
-        fetch(n).start()
-
     for n in range(rings - 2):
-        pl.when(n < count)(functools.partial(fetch_both, n))
+        pl.when(n < count)(lambda n=n: fetch_index(n).start())
     at = [sum(rows[:n]) for n in range(len(rows) + 1)]
     for j, piece in enumerate(pieces):
         lanes = slice(j * part, (j + 1) * part)
@@ -483,51 +498,16 @@
         recv_terms[pl.ds(j, nodes, stride=parts), :] = (
             0.5 * terms[:, j * LANES:(j + 1) * LANES]
         )
-    if halo_turn:
-        out_ref[...] = start_ref[...]
-    else:
-        out_ref[...] = jnp.zeros_like(out_ref)
-
-    def gather(n, rows_held):
+    out_ref[...] = jnp.zeros_like(out_ref)
+
+    def gather(n, held):
         slot = lax.rem(n, rings)
-        for i in range(unit):
+        for i in range(UNIT):
             place = pl.multiple_of(index[slot, i // LANES, i % LANES], parts)
-            rows_held[pl.ds(parts * i, parts), :] = recv_terms[pl.ds(place, parts), :]
-
-    def activate(n, turn, rows_held):
-        start = pl.multiple_of(list_ref[n] * unit, unit)
-        mine = slice(turn * unit, (turn + 1) * unit)
-        before = jnp.dot(
-            held[lax.rem(n, rings)], sender_all[...], preferred_element_type=jnp.float32
-        )
-        before += lax.dot_general(
-            features_ref[:, pl.ds(start, unit)], feature_all[:components, :],
-            (((0,), (0,)), ((), ())),
-            preferred_element_type=jnp.float32,
-        )
-        for j in range(parts):
-            lanes = slice(j * LANES, (j + 1) * LANES)
-            hidden[mine, lanes] = silu_of_double(
-                before[:, lanes] + rows_held[pl.ds(j, unit, stride=parts), :]
-            ).astype(jnp.bfloat16)
-
-    def add_up(first, number):
-        each = lax.broadcasted_iota(jnp.int32, (nodes, LANES), 0)
-        by_node = jnp.concatenate(
-            [
-                jnp.where(
-                    each == recv_ref[pl.ds(list_ref[first + n] * (unit // LANES) + b, 1), :],
-                    1.0,
-                    0.0,
-                )
-                for n in range(number)
-                for b in range(unit // LANES)
-            ],
-            axis=1,
-        ).astype(jnp.bfloat16)
-        out_ref[...] += jnp.dot(
-            by_node, hidden[:number * unit, :], preferred_element_type=jnp.float32
-        )
+            held[pl.ds(parts * i, parts), :] = recv_terms[pl.ds(place, parts), :]
+
+    def found(n):
+        return found_ref[pl.ds(pl.multiple_of(n * UNIT, UNIT), UNIT), :]
 
     @pl.when(count > 0)
     def _():
@@ -538,62 +518,167 @@
         first, second = 2 * m, 2 * m + 1
         after = second + 1 < count
         for n in (first, second):
-            pl.when(n + rings - 2 < count)(functools.partial(fetch_both, n + rings - 2))
+            pl.when(n + rings - 2 < count)(lambda n=n: fetch_index(n + rings - 2).start())
         fetch_index(second).wait()
-        fetch(first).wait()
         gather(second, odd)
-        activate(first, 0, even)
+        activate(first, 0, found(first), even)
         pl.when(after)(lambda: fetch_index(second + 1).wait())
-        fetch(second).wait()
         gather(jnp.where(after, second + 1, second), even)
-        activate(second, 1, odd)
-        add_up(first, 2)
+        activate(second, 1, found(second), odd)
+        add_up(first, 0, 2)
         return carry
 
     lax.fori_loop(0, count // 2, pair, 0)
 
     @pl.when(lax.rem(count, 2) == 1)
     def _():
-        fetch(count - 1).wait()
-        activate(count - 1, 0, even)
-        add_up(count - 1, 1)
-
-
-def node_sums(bounds, found, place, recv, features, start, pieces, rows, columns, nodes,
-              halo_turn):
-    edges, width = found.shape
-    unit = UNIT
+        activate(count - 1, 0, found(count - 1), even)
+        add_up(count - 1, 0, 1)
+
+
+def first_sums(bounds, found, place, recv, features, pieces, rows, columns, nodes):
+    width = found.shape[1]
     units = place.shape[0] // 8
     parts = width // LANES
     vmem = pl.BlockSpec(memory_space=pltpu.VMEM)
     smem = pl.BlockSpec(memory_space=pltpu.SMEM)
     hbm = pl.BlockSpec(memory_space=pltpu.HBM)
+    edges = found.shape[0]
     return pl.pallas_call(
-        functools.partial(edge_kernel, columns, halo_turn, rows),
-        in_specs=[smem, hbm, hbm, vmem, vmem, vmem] + [vmem] * len(pieces),
-        out_specs=vmem,
-        out_shape=jax.ShapeDtypeStruct((nodes, width), jnp.float32),
+        functools.partial(edge_kernel, columns, rows),
+        in_specs=[smem, vmem, hbm, vmem, vmem] + [vmem] * len(pieces),
+        out_specs=[vmem] * 4,
+        out_shape=[
+            jax.ShapeDtypeStruct((nodes, width), jnp.float32),
+            jax.ShapeDtypeStruct((width, width), jnp.bfloat16),
+            jax.ShapeDtypeStruct((nodes * parts, LANES), jnp.float32),
+            jax.ShapeDtypeStruct((rows[3], width), jnp.bfloat16),
+        ],
         scratch_shapes=[
             pltpu.SMEM((units + 1,), jnp.int32),
             pltpu.SMEM((6, 8, LANES), jnp.int32),
             pltpu.VMEM((width, width), jnp.bfloat16),
-            pltpu.VMEM((width, width), jnp.bfloat16),
-            pltpu.VMEM((nodes * parts, LANES), jnp.float32),
-            pltpu.VMEM((rows[3], width), jnp.bfloat16),
-            pltpu.VMEM((unit * parts, LANES), jnp.float32),
-            pltpu.VMEM((unit * parts, LANES), jnp.float32),
-            pltpu.VMEM((6, unit, width), jnp.bfloat16),
-            pltpu.VMEM((2 * unit, width), jnp.bfloat16),
-            pltpu.SemaphoreType.DMA((6,)),
+            pltpu.VMEM((UNIT * parts, LANES), jnp.float32),
+            pltpu.VMEM((UNIT * parts, LANES), jnp.float32),
+            pltpu.VMEM((2 * UNIT, width), jnp.bfloat16),
             pltpu.SemaphoreType.DMA((6,)),
         ],
         compiler_params=pltpu.CompilerParams(vmem_limit_bytes=40 << 20),
         cost_estimate=pl.CostEstimate(
-            flops=edges * width * (width + 2 * nodes) // 2,
-            bytes_accessed=edges * width // 2,
-            transcendentals=edges * width // 4,
+            flops=2 * edges * width * (width + nodes),
+            bytes_accessed=edges * width,
+            transcendentals=edges * width,
         ),
-    )(bounds, found, place, recv, features, start, *pieces)
+    )(bounds, found, place, recv, features, *pieces)
+
+
+def later_kernel(
+    columns,
+    bounds_ref,
+    send_ref,
+    x_ref,
+    halo_ref,
+    embed_ref,
+    bias_ref,
+    place_ref,
+    recv_ref,
+    features_ref,
+    start_ref,
+    sender_all,
+    recv_terms,
+    feature_all,
+    out_ref,
+    *refs,
+):
+    scratch = refs[:POINT_SCRATCH]
+    (place_even, place_odd, rows_even, rows_odd, terms_even, terms_odd, hidden,
+     place_sem) = refs[POINT_SCRATCH:]
+    parts = out_ref.shape[1] // LANES
+    places, rows, terms = (
+        (place_even, place_odd), (rows_even, rows_odd), (terms_even, terms_odd)
+    )
+    count, list_ref, bring, gather, leave, next_index = point_tools(
+        columns, True, bounds_ref, send_ref, x_ref, halo_ref, embed_ref, bias_ref, scratch
+    )
+    activate, add_up = sum_tools(
+        list_ref, features_ref, recv_ref, sender_all, feature_all, hidden, out_ref
+    )
+
+    def place_copy(n, turn):
+        return pltpu.make_async_copy(
+            place_ref.at[index_rows(list_ref[n]), :], places[turn], place_sem.at[turn]
+        )
+
+    for n in range(2):
+        pl.when(n < count)(lambda n=n: place_copy(n, n).start())
+    out_ref[...] = start_ref[...]
+    rows_odd[...] = jnp.zeros_like(rows_odd)
+    terms_odd[...] = jnp.zeros_like(terms_odd)
+
+    def gather_terms(turn):
+        for i in range(UNIT):
+            place = pl.multiple_of(places[turn][i // LANES, i % LANES], parts)
+            terms[turn][pl.ds(parts * i, parts), :] = recv_terms[pl.ds(place, parts), :]
+
+    def one_unit(n, turn):
+        bring(n, turn)
+        place_copy(n, turn).wait()
+        gather(turn, 0)
+        gather(turn, 1)
+        before = jnp.maximum(n - 1, 0)
+        activate(before, 0, rows[1 - turn][...], terms[1 - turn])
+        leave(0, rows[turn], 0)
+        leave(1, rows[turn], CHUNK)
+        gather_terms(turn)
+        add_up(before, 0, 1, n > 0)
+        next_index(n, turn)
+        pl.when(n + 2 < count)(lambda: place_copy(n + 2, turn).start())
+
+    def two_units(m, carry):
+        one_unit(2 * m, 0)
+        pl.when(2 * m + 1 < count)(lambda: one_unit(2 * m + 1, 1))
+        return carry
+
+    lax.fori_loop(0, (count + 1) // 2, two_units, 0)
+    for turn in range(2):
+        @pl.when(jnp.logical_and(count > 0, lax.rem(count - 1, 2) == turn))
+        def _(turn=turn):
+            activate(count - 1, 0, rows[turn][...], terms[turn])
+            add_up(count - 1, 0, 1)
+
+
+def later_sums(bounds, send, points, halo, embed_weight, embed_bias, place, recv, features,
+               start, sender_all, recv_terms, feature_all):
+    channels, width = embed_weight.shape
+    columns = points.shape[1] // LAT
+    units = send.shape[0] // 8
+    parts = width // LANES
+    vmem = pl.BlockSpec(memory_space=pltpu.VMEM)
+    smem = pl.BlockSpec(memory_space=pltpu.SMEM)
+    hbm = pl.BlockSpec(memory_space=pltpu.HBM)
+    return pl.pallas_call(
+        functools.partial(later_kernel, columns),
+        in_specs=[smem] + [hbm] * 6 + [vmem] * 6,
+        out_specs=vmem,
+        out_shape=jax.ShapeDtypeStruct(start.shape, jnp.float32),
+        scratch_shapes=point_scratch(units, channels, width) + [
+            pltpu.SMEM((8, LANES), jnp.int32),
+            pltpu.SMEM((8, LANES), jnp.int32),
+            pltpu.VMEM((UNIT, width), jnp.bfloat16),
+            pltpu.VMEM((UNIT, width), jnp.bfloat16),
+            pltpu.VMEM((UNIT * parts, LANES), jnp.float32),
+            pltpu.VMEM((UNIT * parts, LANES), jnp.float32),
+            pltpu.VMEM((UNIT, width), jnp.bfloat16),
+            pltpu.SemaphoreType.DMA((2,)),
+        ],
+        compiler_params=pltpu.CompilerParams(vmem_limit_bytes=40 << 20),
+        cost_estimate=pl.CostEstimate(
+            flops=units * UNIT * width * (channels + width),
+            bytes_accessed=units * UNIT * width,
+            transcendentals=units * UNIT * width,
+        ),
+    )(bounds, send, points, halo, embed_weight, embed_bias.reshape(1, -1), place, recv,
+      features, start, sender_all, recv_terms, feature_all)
 
 
 def swap_kernel(own_ref, far_ref, own_out, far_out, send, recv):
@@ -669,10 +754,18 @@
             device_id={"ch": partner}, device_id_type=pl.DeviceIdType.MESH,
         )
 
+    half = part // 2
+    halves = [pl.ds(n * half, half) for n in range(2)]
     nears = [
-        copy_to(totals_ref.at[block], near.at[n], near_send.at[n], near_recv.at[n], beside)
-        for n, block in enumerate((partners[2], beside))
+        copy_to(
+            totals_ref.at[partners[2], some, :], near.at[0, some, :], near_send.at[n],
+            near_recv.at[n], beside,
+        )
+        for n, some in enumerate(halves)
     ]
+    nears.append(
+        copy_to(totals_ref.at[beside], near.at[1], near_send.at[2], near_recv.at[2], beside)
+    )
     for copy in nears:
         copy.start()
     at = [sum(rows[:n]) for n in range(len(rows) + 1)]
@@ -680,10 +773,18 @@
         for j in range(parts):
             first = at[4] + j * width
             messages[n, :, j * width:(j + 1) * width] = pieces[n][first:first + width, :]
-    nears[0].wait()
-    onward[...] = (totals_ref[opposite] + swapped(near[0], 1, width)).astype(onward.dtype)
-    pass_on = copy_to(onward, far, far_send.at[0], far_recv.at[0], opposite)
-    pass_on.start()
+    pass_on = []
+    for n, some in enumerate(halves):
+        nears[n].wait()
+        onward[some, :] = (
+            totals_ref[opposite, some, :] + swapped(near[0, some, :], 1, width)
+        ).astype(onward.dtype)
+        pass_on.append(
+            copy_to(
+                onward.at[some, :], far.at[some, :], far_send.at[n], far_recv.at[n], opposite
+            )
+        )
+        pass_on[n].start()
 
     def tally(n, counts):
         nodes_here = lax.broadcasted_iota(jnp.int32, (part, LANES), 0) + me * part
@@ -696,9 +797,10 @@
         0, recv_ref.shape[0] // 8, tally, jnp.zeros((part, LANES), jnp.float32)
     )
     aggregated = jnp.sum(counts, axis=1, keepdims=True) * message_bias_ref[...]
-    nears[1].wait()
+    nears[2].wait()
     sums = totals_ref[me] + swapped(near[1], 1, width)
-    pass_on.wait()
+    for copy in pass_on:
+        copy.wait()
     sums = sums + swapped(far[...].astype(jnp.float32), 2, width)
     for n in range(parts):
         rest = sums[:, n * width:(n + 1) * width]
@@ -752,10 +854,10 @@
             pltpu.VMEM((part, full), jnp.bfloat16),
             pltpu.VMEM((ch_count, part, width), jnp.float32),
             pltpu.VMEM((ch_count - 1, part, width), jnp.bfloat16),
+            pltpu.SemaphoreType.DMA((3,)),
+            pltpu.SemaphoreType.DMA((3,)),
             pltpu.SemaphoreType.DMA((2,)),
             pltpu.SemaphoreType.DMA((2,)),
-            pltpu.SemaphoreType.DMA((1,)),
-            pltpu.SemaphoreType.DMA((1,)),
             pltpu.SemaphoreType.DMA((ch_count - 1,)),
             pltpu.SemaphoreType.DMA((ch_count - 1,)),
             pltpu.VMEM((ch_count, width, full), jnp.bfloat16),
@@ -812,15 +914,14 @@
     beside, diagonal = swapped_beside(packed, opposite)
     pieces = [packed, beside, opposite, diagonal]
 
-    totals = jnp.zeros((8, LANES), jnp.float32)
-    for halo_turn in (False, True):
-        found = gathered(
-            bounds, send, points, halo if halo_turn else None, embed_weight, embed_bias,
-            halo_turn,
-        )
-        totals = node_sums(
-            bounds, found, place, recv, edge_features, totals, pieces, rows, columns, mesh_nodes, halo_turn,
-        )
+    found = gathered(bounds, send, points, embed_weight, embed_bias)
+    totals, *prepared_weights = first_sums(
+        bounds, found, place, recv, edge_features, pieces, rows, columns, mesh_nodes
+    )
+    totals = later_sums(
+        bounds, send, points, halo, embed_weight, embed_bias, place, recv, edge_features,
+        totals, *prepared_weights,
+    )
     return finished(
         totals, recv, message_bias, pieces, rows, mesh_nodes
     )

time: 69.4 us -> 66.8 us (0.963)
  Pallas kernels: 60.6 us -> 57.1 us
  waiting for transfers between devices: 1.2 us -> 2.17 us
    pallas_call x4 -> x3, Pallas kernels: 39.4 us -> 37.2 us  [the longest x1 14.6 us: later_sums(): pl.pallas_call(functools.partial(later_kernel, columns), in_specs=[smem]...]
  transfers between devices with their start and end apart: 2 -> 2, of which waited for: 1 -> 2; matrix products, arithmetic and copies ran while one was open for 0% -> 0% of each run, Pallas kernels for 41% -> 41%
where the time goes in v3:
time: 66.8 us; the launch traced here: 66.6 us
  Pallas kernels  57.1 us (85%)
  starting transfers between devices  4.95 us (7%)
  local copies, waits for them, and re-layouts  2.27 us (3%)
  waiting for transfers between devices  2.17 us (3%)
    pallas_call x1, Pallas kernels, later_sums(): pl.pallas_call(functools.partial(later_kernel, columns), in_specs=[smem]...  14.6 us
    pallas_call x1, Pallas kernels, first_sums(): pl.pallas_call(functools.partial(edge_kernel, columns, rows), in_specs=[s...  11.5 us
    pallas_call x1, Pallas kernels, finished(): pl.pallas_call(functools.partial(tail_kernel, rows), in_specs=[vmem] * (3...  11.2 us
    pallas_call x1, Pallas kernels, gathered(): pl.pallas_call(functools.partial(gather_kernel, columns), in_specs=[smem,...  11.1 us
    ppermute x1, starting transfers between devices, on_device(): halo = lax.ppermute(edge_columns, ('lon', 'ch'), hops)  4.88 us
    pallas_call x1, Pallas kernels, swapped_beside(): pl.pallas_call(swap_kernel, in_specs=[vmem] * 2, out_specs=[vmem] * 2, ou...  4.59 us
    pallas_call x1, Pallas kernels, prepared(): pl.pallas_call(functools.partial(prepare_kernel, columns), in_specs=[hbm]...  4.06 us
    unnamed x19, local copies, waits for them, and re-layouts  2.27 us
  transfers between devices with their start and end apart: 2, of which 2 were waited for; matrix products, arithmetic and copies ran while one was open for 0% of the time, Pallas kernels for 41%

profile of v3, /device:TPU:0, one launch (start us, length us, event | category | flops | bytes accessed | tf_op | source)
XLA Modules:
  0.0 66.6 jit_solution(1033688853753164161)
XLA Ops:
  0.0 0.0 copy-start.3
  0.0 0.0 copy-start.7
  0.0 4.1 %shard_map.145 = (bf16[474,2560]{1,0:T(8,128)(2,1)}, bf16[2192,128]{1,0:T(8,128)(2,1)}, s32[352,128]{1,0:T(8,128)}, s32[176,128]{1,0:T(8,128)}, s32[352,128]{1,0:T(8,128)}, /*index=5*/s32[2,256]{1,0:T(2,128)}) custom-call(bf16[474,28800]{1,0:T(8,128)(2,1)} %bitcast.13, s32[176,128]{1,0:T(8,128)} %bitcast.16, s32[176,128]{1,0:T(8,128)} %bitcast.17, ...), custom_call_target="tpu_custom_call" | custom-call | tf_op jit(solution)/shard_map/pallas_call | solution.py:188
  4.1 4.9 %collective-permute-start = (bf16[474,2560]{1,0:T(8,128)(2,1)}, bf16[474,2560]{1,0:T(8,128)(2,1)S(1)}, u32[]{:S(2)}, u32[]{:S(2)}) collective-permute-start(bf16[474,2560]{1,0:T(8,128)(2,1)} %get-tuple-element.19), channel_id=1, source_target_pairs={{0,4},{3,31},{4,8},{7,3},{8,12},{11,7},{12,16},{15,11},{16,20},{19... | collective-permute-start | bytes 7280648 | tf_op jit(solution)/shard_map/ppermute | solution.py:911
  9.0 0.1 collective-permute-start.1
  9.0 0.0 copy-done.3
  9.0 0.0 copy-done.7
  9.1 0.0 copy-start.5
  9.1 0.9 %copy-done.5 = s32[352,128]{1,0:T(8,128)S(1)} copy-done((s32[352,128]{1,0:T(8,128)S(1)}, s32[352,128]{1,0:T(8,128)}, u32[]{:S(2)}) %copy-start.5) | copy-done | bytes 180248
  10.0 0.0 copy-start.8
  10.0 0.7 copy-done.8
  10.6 0.0 copy-start
  10.6 0.0 copy-start.1
  10.6 0.0 copy-start.4
  10.6 0.0 copy-start.6
  10.7 11.1 %shard_map.146.found_ref = bf16[3840,512]{1,0:T(8,128)(2,1)S(1)} custom-call(s32[2,256]{1,0:T(2,128)S(1)} %copy-done.8, s32[352,128]{1,0:T(8,128)S(1)} %copy-done.5, bf16[474,28800]{1,0:T(8,128)(2,1)} %bitcast.14, bf16[474,512]{1,0:T(8,128)(2,1)S(1)} %copy-done.3, f32[1,512]{1,0:T(1,128)S(1)} %bitcast.11), custom_call_target="tpu_custom_call" | custom-call | flops 10934550528 | bytes 11534336 | tf_op jit(solution)/shard_map/pallas_call | solution.py:394
  21.7 1.7 %collective-permute-done.1.far_ref.refs_2_ = bf16[2192,128]{1,0:T(8,128)(2,1)S(1)} collective-permute-done((bf16[2192,128]{1,0:T(8,128)(2,1)}, bf16[2192,128]{1,0:T(8,128)(2,1)S(1)}, u32[]{:S(2)}, u32[]{:S(2)}) %collective-permute-start.1) | collective-permute-done | bytes 561184 | tf_op jit(solution)/shard_map/ppermute | solution.py:913
  23.4 0.0 copy-done
  23.4 4.6 %shard_map.147 = (bf16[2192,128]{1,0:T(8,128)(2,1)S(1)}, bf16[2192,128]{1,0:T(8,128)(2,1)S(1)}) custom-call(bf16[2192,128]{1,0:T(8,128)(2,1)S(1)} %copy-done, bf16[2192,128]{1,0:T(8,128)(2,1)S(1)} %collective-permute-done.1.far_ref.refs_2_), custom_call_target="tpu_custom_call" | custom-call | tf_op jit(solution)/shard_map/pallas_call | solution.py:706
  28.0 0.0 copy-done.1
  28.0 0.0 copy-done.4
  28.0 0.0 copy-done.6
  28.0 11.5 %shard_map.148 = (f32[640,512]{1,0:T(8,128)S(1)}, bf16[512,512]{1,0:T(8,128)(2,1)S(1)}, f32[2560,128]{1,0:T(8,128)S(1)}, bf16[16,512]{1,0:T(8,128)(2,1)S(1)}) custom-call(s32[2,256]{1,0:T(2,128)S(1)} %copy-done.8, bf16[3840,512]{1,0:T(8,128)(2,1)S(1)} %shard_map.146.found_ref, s32[352,128]{1,0:T(8,128)S(1)} %copy-done.6, s32[176,128]{1,0:T(8,128)S(1)} %copy-done.1, ...), custom_call_target="tpu_custom_call" | custom-call | flops 4529848320 | bytes 1966080 | tf_op jit(solution)/shard_map/pallas_call | solution.py:547
  39.6 0.5 collective-permute-done.halo_ref
  40.1 0.0 copy-start.2
  40.1 14.6 %shard_map.149 = f32[640,512]{1,0:T(8,128)S(1)} custom-call(s32[2,256]{1,0:T(2,128)S(1)} %copy-done.8, s32[352,128]{1,0:T(8,128)S(1)} %copy-done.5, bf16[474,28800]{1,0:T(8,128)(2,1)} %bitcast.15, bf16[474,2560]{1,0:T(8,128)(2,1)S(1)} %collective-permute-done.halo_ref, bf16[474,512]{1,0:T(8,128)(2,1)S(1)} %copy-done.3, f32[1,512]{1,0:T(1,128)S(1)} %bitcast.12, ...), custom_call_target="tpu_custom_call" | custom-call | flops 11372855296 | bytes 11534336 | tf_op jit(solution)/shard_map/pallas_call | solution.py:659
  54.7 0.0 copy-done.2
  54.7 11.2 %shard_map.150 = bf16[640,128]{1,0:T(8,128)(2,1)S(1)} custom-call(f32[4,160,512]{2,1,0:T(8,128)S(1)} %bitcast.9, s32[176,128]{1,0:T(8,128)S(1)} %copy-done.1, f32[1,512]{1,0:T(1,128)S(1)} %bitcast.10, bf16[2192,128]{1,0:T(8,128)(2,1)S(1)} %copy-done, bf16[2192,128]{1,0:T(8,128)(2,1)S(1)} %get-tuple-element.23.refs_1_, ...), custom_call_target="tpu_custom_call" | custom-call | tf_op jit(solution)/shard_map/pallas_call | solution.py:846
  65.9 0.7 %copy.17 = bf16[640,128]{1,0:T(8,128)(2,1)} copy(bf16[640,128]{1,0:T(8,128)(2,1)S(1)} %shard_map.150) | data formatting | bytes 327680
Async XLA Ops:
  0.0 9.0 %copy-start.3 = (bf16[474,512]{1,0:T(8,128)(2,1)S(1)}, bf16[474,512]{1,0:T(8,128)(2,1)}, u32[]{:S(2)}) copy-start(bf16[474,512]{1,0:T(8,128)(2,1)} %embed_ref.3) | copy-start | bytes 1456132
  0.0 9.0 %copy-start.7 = (f32[512]{0:T(512)S(1)}, f32[512]{0:T(512)}, u32[]{:S(2)}) copy-start(f32[512]{0:T(512)} %param.17) | copy-start | bytes 6148
  4.1 36.0 %collective-permute-start = (bf16[474,2560]{1,0:T(8,128)(2,1)}, bf16[474,2560]{1,0:T(8,128)(2,1)S(1)}, u32[]{:S(2)}, u32[]{:S(2)}) collective-permute-start(bf16[474,2560]{1,0:T(8,128)(2,1)} %get-tuple-element.19), channel_id=1, source_target_pairs={{0,4},{3,31},{4,8},{7,3},{8,12},{11,7},{12,16},{15,11},{16,20},{19... | collective-permute-start | bytes 7280648 | tf_op jit(solution)/shard_map/ppermute | solution.py:911
  9.0 14.5 %collective-permute-start.1 = (bf16[2192,128]{1,0:T(8,128)(2,1)}, bf16[2192,128]{1,0:T(8,128)(2,1)S(1)}, u32[]{:S(2)}, u32[]{:S(2)}) collective-permute-start(bf16[2192,128]{1,0:T(8,128)(2,1)} %get-tuple-element.22.own_ref.refs_0_), channel_id=1, source_target_pairs={{0,2},{1,3},{2,0},{3,1},{4,6},{5,7},{6,4},{7,5},{8,10},{9,11},{10,... | collective-permute-start | bytes 1683464 | tf_op jit(solution)/shard_map/ppermute | solution.py:913
  9.1 0.9 %copy-start.5 = (s32[352,128]{1,0:T(8,128)S(1)}, s32[352,128]{1,0:T(8,128)}, u32[]{:S(2)}) copy-start(s32[352,128]{1,0:T(8,128)} %get-tuple-element.18.send_ref) | copy-start | bytes 540676
  10.0 0.7 copy-start.8
  10.6 12.8 %copy-start = (bf16[2192,128]{1,0:T(8,128)(2,1)S(1)}, bf16[2192,128]{1,0:T(8,128)(2,1)}, u32[]{:S(2)}) copy-start(bf16[2192,128]{1,0:T(8,128)(2,1)} %get-tuple-element.22.own_ref.refs_0_) | copy-start | bytes 1683460
  10.6 17.4 %copy-start.1 = (s32[176,128]{1,0:T(8,128)S(1)}, s32[176,128]{1,0:T(8,128)}, u32[]{:S(2)}) copy-start(s32[176,128]{1,0:T(8,128)} %get-tuple-element.21.recv_ref) | copy-start | bytes 270340
  10.6 17.4 %copy-start.4 = (bf16[4,22528]{1,0:T(4,128)(2,1)S(1)}, bf16[4,22528]{1,0:T(4,128)(2,1)}, u32[]{:S(2)}) copy-start(bf16[4,22528]{1,0:T(4,128)(2,1)} %features_ref.3) | copy-start | bytes 540676
  10.6 17.4 %copy-start.6 = (s32[352,128]{1,0:T(8,128)S(1)}, s32[352,128]{1,0:T(8,128)}, u32[]{:S(2)}) copy-start(s32[352,128]{1,0:T(8,128)} %get-tuple-element.20.place_ref) | copy-start | bytes 540676
  40.1 14.6 %copy-start.2 = (f32[512]{0:T(512)S(1)}, f32[512]{0:T(512)}, u32[]{:S(2)}) copy-start(f32[512]{0:T(512)} %param.27) | copy-start | bytes 6148

commit v4 on v3

--- a/solution.py
+++ b/solution.py
@@ -76,18 +76,8 @@
         ref[16 * n + 8:16 * n + 16, :] = pltpu.roll(tile, 4, 0)
 
 
-def prepare_kernel(
-    columns,
-    x_ref,
-    *refs,
-):
-    sources, refs = refs[:10], refs[10:]
-    (edge_ref, packed_ref, send_ref, recv_ref, place_ref, bounds_ref, buffer, packed,
-     senders_ref, receivers_ref, feature_ref, bias_ref, gain_ref, shift_ref,
-     in_sem, out_sem, pack_sem, source_sem) = refs
-    lon_count = lax.axis_size("lon")
-    lon_place, ch_place = lax.axis_index("lon"), lax.axis_index("ch")
-    start = jnp.where(ch_place == 0, (columns - HALO) * LAT, 0)
+def cut_kernel(columns, x_ref, edge_ref, buffer, in_sem, out_sem):
+    start = jnp.where(lax.axis_index("ch") == 0, (columns - HALO) * LAT, 0)
     takes = [
         pltpu.make_async_copy(
             x_ref.at[:, pl.ds(pl.multiple_of(start + n * LAT, LANES), LAT)],
@@ -102,6 +92,40 @@
         )
         for n in range(HALO)
     ]
+    for take in takes:
+        take.start()
+    for take, give in zip(takes, gives):
+        take.wait()
+        give.start()
+    for give in gives:
+        give.wait()
+
+
+def cut_columns(points):
+    hbm = pl.BlockSpec(memory_space=pltpu.HBM)
+    return pl.pallas_call(
+        functools.partial(cut_kernel, points.shape[1] // LAT),
+        in_specs=[hbm],
+        out_specs=hbm,
+        out_shape=jax.ShapeDtypeStruct((points.shape[0], HALO * LAT), points.dtype),
+        scratch_shapes=[
+            pltpu.VMEM((HALO, points.shape[0], LAT), points.dtype),
+            pltpu.SemaphoreType.DMA((HALO,)),
+            pltpu.SemaphoreType.DMA((HALO,)),
+        ],
+        compiler_params=pltpu.CompilerParams(vmem_limit_bytes=40 << 20),
+    )(points)
+
+
+def prepare_kernel(
+    columns,
+    *refs,
+):
+    sources, refs = refs[:10], refs[10:]
+    (packed_ref, send_ref, recv_ref, place_ref, bounds_ref, packed,
+     senders_ref, receivers_ref, feature_ref, bias_ref, gain_ref, shift_ref,
+     pack_sem, source_sem) = refs
+    lon_count, lon_place = lax.axis_size("lon"), lax.axis_index("lon")
     targets = [senders_ref, receivers_ref]
     row = 0
     for ref in sources[2:5]:
@@ -121,11 +145,8 @@
         )
         for n in range(sources[9].shape[1] // part)
     ]
-    for copy in takes + loads:
+    for copy in loads:
         copy.start()
-    for take, give in zip(takes, gives):
-        take.wait()
-        give.start()
     for copy in loads:
         copy.wait()
     singles = [feature_ref[...].astype(jnp.float32)]
@@ -166,15 +187,12 @@
             [best, jnp.full((tall - best.shape[0], LANES), fill, jnp.int32)]
         )
         bounds_ref[n:n + 1, :] = pick(jnp.transpose(best), axis=0, keepdims=True)
-    for give in gives:
-        give.wait()
     pack.wait()
 
 
-def prepared(points, senders, receivers, sender_weight, receiver_weight, mesh_latent,
+def prepared(columns, senders, receivers, sender_weight, receiver_weight, mesh_latent,
              feature_weight, hidden_bias, norm_gain, norm_shift, message_weight):
-    columns = points.shape[1] // LAT
-    assert LAT == 5 * LANES and lax.axis_size("lon") * points.shape[1] // LANES < 40960
+    assert LAT == 5 * LANES and lax.axis_size("lon") * columns * LAT // LANES < 40960
     rows = senders.shape[0] // LANES
     part = sender_weight.shape[1]
     packed_rows = (
@@ -187,10 +205,9 @@
     assert rows % 8 == 0 and UNIT == 4 * LANES
     return pl.pallas_call(
         functools.partial(prepare_kernel, columns),
-        in_specs=[hbm] * 11,
-        out_specs=[hbm, hbm, vmem, vmem, vmem, vmem],
+        in_specs=[hbm] * 10,
+        out_specs=[hbm, vmem, vmem, vmem, vmem],
         out_shape=[
-            jax.ShapeDtypeStruct((points.shape[0], HALO * LAT), points.dtype),
             jax.ShapeDtypeStruct((packed_rows, part), jnp.bfloat16),
             wide_ids,
             ids,
@@ -198,7 +215,6 @@
             jax.ShapeDtypeStruct((2, -(-rows // LANES) * LANES), jnp.int32),
         ],
         scratch_shapes=[
-            pltpu.VMEM((HALO, points.shape[0], LAT), points.dtype),
             pltpu.VMEM((packed_rows, part), jnp.bfloat16),
             pltpu.VMEM((rows, LANES), jnp.int32),
             pltpu.VMEM((rows, LANES), jnp.int32),
@@ -206,13 +222,11 @@
             pltpu.VMEM((1, part), jnp.float32),
             pltpu.VMEM((1, part), jnp.float32),
             pltpu.VMEM((1, part), jnp.float32),
-            pltpu.SemaphoreType.DMA((HALO,)),
-            pltpu.SemaphoreType.DMA((HALO,)),
             pltpu.SemaphoreType.DMA,
             pltpu.SemaphoreType.DMA((9 + PARTS,)),
         ],
-        compiler_params=pltpu.CompilerParams(vmem_limit_bytes=63 << 20),
-    )(points, senders.reshape(rows, LANES), receivers.reshape(rows, LANES), sender_weight,
+        compiler_params=pltpu.CompilerParams(vmem_limit_bytes=40 << 20),
+    )(senders.reshape(rows, LANES), receivers.reshape(rows, LANES), sender_weight,
       receiver_weight, mesh_latent, feature_weight, hidden_bias.reshape(1, -1),
       norm_gain.reshape(1, -1), norm_shift.reshape(1, -1), message_weight)
 
@@ -261,28 +275,10 @@
         copy.start()
     count = pick_units(bounds_ref, list_ref, list_ref.shape[0] - 1, columns, later)
 
-    for n in range(SLOTS):
-        held_column[n] = -1
-
-    def note_unit(n, total):
-        u = list_ref[n]
-        event_at[n] = total
-
-        def note(column, total):
-            slot = lax.rem(column, SLOTS)
-            new = jnp.where(held_column[slot] == column, 0, 1)
-            held_column[slot] = column
-            events[total] = column
-            return total + new
-
-        return lax.fori_loop(low_of(bounds_ref, u), high_of(bounds_ref, u) + 1, note, total)
-
-    total = lax.fori_loop(0, count, note_unit, jnp.int32(0))
-    event_at[count] = total
-
     def fetch(event):
-        column, slot = events[event], lax.rem(event, depth)
-
+        bring_in(events[event], lax.rem(event, depth))
+
+    def bring_in(column, slot):
         def copy(source, place):
             start = pl.multiple_of(place * LAT, LANES)
             return pltpu.make_async_copy(
@@ -299,6 +295,26 @@
         )
         pl.when(jnp.logical_not(outside))(lambda: copy(x_ref, column - HALO).start())
 
+    pl.when(count > 0)(lambda: bring_in(low_of(bounds_ref, list_ref[0]), 0))
+    for n in range(SLOTS):
+        held_column[n] = -1
+
+    def note_unit(n, total):
+        u = list_ref[n]
+        event_at[n] = total
+
+        def note(column, total):
+            slot = lax.rem(column, SLOTS)
+            new = jnp.where(held_column[slot] == column, 0, 1)
+            held_column[slot] = column
+            events[total] = column
+            return total + new
+
+        return lax.fori_loop(low_of(bounds_ref, u), high_of(bounds_ref, u) + 1, note, total)
+
+    total = lax.fori_loop(0, count, note_unit, jnp.int32(0))
+    event_at[count] = total
+
     def index_copy(n, turn):
         return pltpu.make_async_copy(
             send_ref.at[index_rows(list_ref[n]), :], index[turn], index_sem.at[turn]
@@ -308,7 +324,7 @@
         fetch(event)
         return carry
 
-    lax.fori_loop(0, jnp.minimum(total, depth), fetch_first, 0)
+    lax.fori_loop(1, jnp.minimum(total, depth), fetch_first, 0)
     for n in range(2):
         pl.when(n < count)(lambda n=n: index_copy(n, n).start())
     for copy in weights:
@@ -897,8 +913,9 @@
     assert edges % unit == 0 and unit == 2 * CHUNK
     points = grid_inputs.T
 
-    edge_columns, packed, send, recv, place, bounds = prepared(
-        points, senders, receivers, sender_weight, receiver_weight, mesh_latent,
+    edge_columns = cut_columns(points)
+    packed, send, recv, place, bounds = prepared(
+        columns, senders, receivers, sender_weight, receiver_weight, mesh_latent,
         feature_weight, hidden_bias, norm_gain, norm_shift, message_weight,
     )
     rows = (width, width, mesh_nodes, 16)

time: 66.8 us -> 64.8 us (0.970)
  Pallas kernels: 57.1 us -> 55.2 us
  local copies, waits for them, and re-layouts: 2.27 us -> 0.73 us
  waiting for transfers between devices: 2.17 us -> 3.44 us
    pallas_call x1, Pallas kernels: 4.06 us -> 1.27 us  [prepared(): pl.pallas_call(functools.partial(prepare_kernel, columns), in_specs=[hbm]...]
    pallas_call x0 -> x1, Pallas kernels: none -> 1.91 us  [cut_columns(): pl.pallas_call(functools.partial(cut_kernel, points.shape[1] // LAT), in_...]
    ppermute x1, waiting for transfers between devices: 1.69 us -> 3.43 us  [on_device(): opposite = lax.ppermute(packed, 'ch', [(i, i ^ 2) for i in range(ch_count)])]
    unnamed x19 -> x29, local copies, waits for them, and re-layouts: 2.27 us -> 0.73 us
  transfers between devices with their start and end apart: 2 -> 2, of which waited for: 2 -> 1; matrix products, arithmetic and copies ran while one was open for 0% -> 0% of each run, Pallas kernels for 41% -> 42%
where the time goes in v4:
time: 64.8 us; the launch traced here: 64.6 us
  Pallas kernels  55.2 us (85%)
  starting transfers between devices  4.98 us (8%)
  waiting for transfers between devices  3.44 us (5%)
  local copies, waits for them, and re-layouts  0.73 us (1%)
    pallas_call x1, Pallas kernels, later_sums(): pl.pallas_call(functools.partial(later_kernel, columns), in_specs=[smem]...  14.6 us
    pallas_call x1, Pallas kernels, first_sums(): pl.pallas_call(functools.partial(edge_kernel, columns, rows), in_specs=[s...  11.5 us
    pallas_call x1, Pallas kernels, finished(): pl.pallas_call(functools.partial(tail_kernel, rows), in_specs=[vmem] * (3...  11.2 us
    pallas_call x1, Pallas kernels, gathered(): pl.pallas_call(functools.partial(gather_kernel, columns), in_specs=[smem,...  10.7 us
    ppermute x1, starting transfers between devices, on_device(): halo = lax.ppermute(edge_columns, ('lon', 'ch'), hops)  4.91 us
    pallas_call x1, Pallas kernels, swapped_beside(): pl.pallas_call(swap_kernel, in_specs=[vmem] * 2, out_specs=[vmem] * 2, ou...  3.95 us
    ppermute x1, waiting for transfers between devices, on_device(): opposite = lax.ppermute(packed, 'ch', [(i, i ^ 2) for i in range(ch_count)])  3.43 us
    pallas_call x1, Pallas kernels, cut_columns(): pl.pallas_call(functools.partial(cut_kernel, points.shape[1] // LAT), in_...  1.91 us
  transfers between devices with their start and end apart: 2, of which 1 were waited for; matrix products, arithmetic and copies ran while one was open for 0% of the time, Pallas kernels for 42%

profile of v4, /device:TPU:0, one launch (start us, length us, event | category | flops | bytes accessed | tf_op | source)
XLA Modules:
  0.0 64.6 jit_solution(17290880723076104834)
XLA Ops:
  0.0 0.0 copy-start.5
  0.0 0.0 copy-start.7
  0.0 0.0 copy-start.8
  0.0 0.0 copy-start.9
  0.1 0.0 copy-start.10
  0.1 0.0 copy-start.11
  0.1 1.9 %shard_map.146 = bf16[474,2560]{1,0:T(8,128)(2,1)S(1)} custom-call(bf16[474,28800]{1,0:T(8,128)(2,1)} %bitcast.18), custom_call_target="tpu_custom_call" | custom-call | tf_op jit(solution)/shard_map/pallas_call | solution.py:106
  2.0 4.9 %collective-permute-start = (bf16[474,2560]{1,0:T(8,128)(2,1)S(1)}, bf16[474,2560]{1,0:T(8,128)(2,1)S(1)}, u32[]{:S(2)}, u32[]{:S(2)}) collective-permute-start(bf16[474,2560]{1,0:T(8,128)(2,1)S(1)} %shard_map.146), channel_id=1, source_target_pairs={{0,4},{3,31},{4,8},{7,3},{8,12},{11,7},{12,16},{15,11},{16,20},{19... | collective-permute-start | bytes 7280648 | tf_op jit(solution)/shard_map/ppermute | solution.py:928
  6.9 0.0 copy-done
  6.9 0.0 copy-done.1
  6.9 0.0 copy-done.2
  7.0 0.0 copy-done.3
  7.0 0.0 copy-done.4
  7.0 0.0 copy-done.5
  7.0 0.0 copy-done.7
  7.0 0.0 copy-done.8
  7.0 0.0 copy-done.9
  7.0 0.0 copy-done.10
  7.0 1.3 %shard_map.145 = (bf16[2192,128]{1,0:T(8,128)(2,1)S(1)}, s32[352,128]{1,0:T(8,128)S(1)}, s32[176,128]{1,0:T(8,128)S(1)}, s32[352,128]{1,0:T(8,128)S(1)}, s32[2,256]{1,0:T(2,128)S(1)}) custom-call(s32[176,128]{1,0:T(8,128)S(1)} %bitcast.10, s32[176,128]{1,0:T(8,128)S(1)} %bitcast.11, bf16[512,128]{1,0:T(8,128)(2,1)S(1)} %copy-done.1, ...), custom_call_target="tpu_custom_call" | custom-call | tf_op jit(solution)/shard_map/pallas_call | solution.py:206
  8.3 0.1 collective-permute-start.1
  8.4 0.0 copy-done.11
  8.4 0.0 copy-done.13
  8.4 0.0 copy-start.12
  8.4 10.7 %shard_map.147.found_ref = bf16[3840,512]{1,0:T(8,128)(2,1)S(1)} custom-call(s32[2,256]{1,0:T(2,128)S(1)} %get-tuple-element.16.bounds_ref, s32[352,128]{1,0:T(8,128)S(1)} %get-tuple-element.17.send_ref, bf16[474,28800]{1,0:T(8,128)(2,1)} %bitcast.19, bf16[474,512]{1,0:T(8,128)(2,1)S(1)} %copy-done.11, f32[1,512]{1,0:T(1,128)S(1)} %bitcast.16), custom_call_target="tpu_custom_call" | custom-call | flops 10934550528 | bytes 11534336 | tf_op jit(solution)/shard_map/pallas_call | solution.py:410
  19.1 3.4 %collective-permute-done.1.far_ref.refs_2_ = bf16[2192,128]{1,0:T(8,128)(2,1)S(1)} collective-permute-done((bf16[2192,128]{1,0:T(8,128)(2,1)S(1)}, bf16[2192,128]{1,0:T(8,128)(2,1)S(1)}, u32[]{:S(2)}, u32[]{:S(2)}) %collective-permute-start.1) | collective-permute-done | bytes 561184 | tf_op jit(solution)/shard_map/ppermute | solution.py:930
  22.5 3.9 %shard_map.148 = (bf16[2192,128]{1,0:T(8,128)(2,1)S(1)}, bf16[2192,128]{1,0:T(8,128)(2,1)S(1)}) custom-call(bf16[2192,128]{1,0:T(8,128)(2,1)S(1)} %get-tuple-element.20.own_ref.refs_0_, bf16[2192,128]{1,0:T(8,128)(2,1)S(1)} %collective-permute-done.1.far_ref.refs_2_), custom_call_target="tpu_custom_call" | custom-call | tf_op jit(solution)/shard_map/pallas_call | solution.py:722
  26.5 11.5 %shard_map.149 = (f32[640,512]{1,0:T(8,128)S(1)}, bf16[512,512]{1,0:T(8,128)(2,1)S(1)}, f32[2560,128]{1,0:T(8,128)S(1)}, bf16[16,512]{1,0:T(8,128)(2,1)S(1)}) custom-call(s32[2,256]{1,0:T(2,128)S(1)} %get-tuple-element.16.bounds_ref, bf16[3840,512]{1,0:T(8,128)(2,1)S(1)} %shard_map.147.found_ref, s32[352,128]{1,0:T(8,128)S(1)} %get-tuple-element.18.place_ref, ...), custom_call_target="tpu_custom_call" | custom-call | flops 4529848320 | bytes 1966080 | tf_op jit(solution)/shard_map/pallas_call | solution.py:563
  38.1 0.0 collective-permute-done.halo_ref
  38.1 0.0 copy-start.6
  38.1 14.6 %shard_map.150 = f32[640,512]{1,0:T(8,128)S(1)} custom-call(s32[2,256]{1,0:T(2,128)S(1)} %get-tuple-element.16.bounds_ref, s32[352,128]{1,0:T(8,128)S(1)} %get-tuple-element.17.send_ref, bf16[474,28800]{1,0:T(8,128)(2,1)} %bitcast.20, bf16[474,2560]{1,0:T(8,128)(2,1)S(1)} %collective-permute-done.halo_ref, bf16[474,512]{1,0:T(8,128)(2,1)S(1)} %copy-done.11, ...), custom_call_target="tpu_custom_call" | custom-call | flops 11372855296 | bytes 11534336 | tf_op jit(solution)/shard_map/pallas_call | solution.py:675
  52.7 11.2 %shard_map.151 = bf16[640,128]{1,0:T(8,128)(2,1)S(1)} custom-call(f32[4,160,512]{2,1,0:T(8,128)S(1)} %bitcast.9, s32[176,128]{1,0:T(8,128)S(1)} %get-tuple-element.19.recv_ref, f32[1,512]{1,0:T(1,128)S(1)} %bitcast.12, bf16[2192,128]{1,0:T(8,128)(2,1)S(1)} %get-tuple-element.20.own_ref.refs_0_, bf16[2192,128]{1,0:T(8,128)(2,1)S(1)} %get-tuple-element.21.refs_1_, ...), custom_call_target="tpu_custom_call" | custom-call | tf_op jit(solution)/shard_map/pallas_call | solution.py:862
  63.9 0.7 %copy.17 = bf16[640,128]{1,0:T(8,128)(2,1)} copy(bf16[640,128]{1,0:T(8,128)(2,1)S(1)} %shard_map.151) | data formatting | bytes 327680
  (8 shorter events, 0.0 us)
Async XLA Ops:
  0.0 6.9 %copy-start = (bf16[640,128]{1,0:T(8,128)(2,1)S(1)}, bf16[640,128]{1,0:T(8,128)(2,1)}, u32[]{:S(2)}) copy-start(bf16[640,128]{1,0:T(8,128)(2,1)} %refs_4_.1) | copy-start | bytes 491524
  0.0 6.9 %copy-start.1 = (bf16[512,128]{1,0:T(8,128)(2,1)S(1)}, bf16[512,128]{1,0:T(8,128)(2,1)}, u32[]{:S(2)}) copy-start(bf16[512,128]{1,0:T(8,128)(2,1)} %refs_2_.1) | copy-start | bytes 393220
  0.0 6.9 %copy-start.2 = (bf16[512,128]{1,0:T(8,128)(2,1)S(1)}, bf16[512,128]{1,0:T(8,128)(2,1)}, u32[]{:S(2)}) copy-start(bf16[512,128]{1,0:T(8,128)(2,1)} %refs_3_.1) | copy-start | bytes 393220
  0.0 6.9 %copy-start.3 = (bf16[128,512]{1,0:T(8,128)(2,1)S(1)}, bf16[128,512]{1,0:T(8,128)(2,1)}, u32[]{:S(2)}) copy-start(bf16[128,512]{1,0:T(8,128)(2,1)} %refs_9_.1) | copy-start | bytes 393220
  0.0 7.0 %copy-start.4 = (s32[22528]{0:T(1024)S(1)}, s32[22528]{0:T(1024)}, u32[]{:S(2)}) copy-start(s32[22528]{0:T(1024)} %param.20) | copy-start | bytes 270340
  0.0 7.0 %copy-start.5 = (s32[22528]{0:T(1024)S(1)}, s32[22528]{0:T(1024)}, u32[]{:S(2)}) copy-start(s32[22528]{0:T(1024)} %param.21) | copy-start | bytes 270340
  0.0 7.0 %copy-start.7 = (bf16[4,128]{1,0:T(4,128)(2,1)S(1)}, bf16[4,128]{1,0:T(4,128)(2,1)}, u32[]{:S(2)}) copy-start(bf16[4,128]{1,0:T(4,128)(2,1)} %refs_5_.1) | copy-start | bytes 3076
  0.0 7.0 %copy-start.8 = (f32[128]{0:T(128)S(1)}, f32[128]{0:T(128)}, u32[]{:S(2)}) copy-start(f32[128]{0:T(128)} %param.25) | copy-start | bytes 1540
  0.0 7.0 %copy-start.9 = (f32[128]{0:T(128)S(1)}, f32[128]{0:T(128)}, u32[]{:S(2)}) copy-start(f32[128]{0:T(128)} %param.28) | copy-start | bytes 1540
  0.1 7.0 %copy-start.10 = (f32[128]{0:T(128)S(1)}, f32[128]{0:T(128)}, u32[]{:S(2)}) copy-start(f32[128]{0:T(128)} %param.29) | copy-start | bytes 1540
  0.1 8.3 %copy-start.11 = (bf16[474,512]{1,0:T(8,128)(2,1)S(1)}, bf16[474,512]{1,0:T(8,128)(2,1)}, u32[]{:S(2)}) copy-start(bf16[474,512]{1,0:T(8,128)(2,1)} %embed_ref.3) | copy-start | bytes 1456132
  0.1 8.3 %copy-start.13 = (f32[512]{0:T(512)S(1)}, f32[512]{0:T(512)}, u32[]{:S(2)}) copy-start(f32[512]{0:T(512)} %param.17) | copy-start | bytes 6148
  2.0 36.1 %collective-permute-start = (bf16[474,2560]{1,0:T(8,128)(2,1)S(1)}, bf16[474,2560]{1,0:T(8,128)(2,1)S(1)}, u32[]{:S(2)}, u32[]{:S(2)}) collective-permute-start(bf16[474,2560]{1,0:T(8,128)(2,1)S(1)} %shard_map.146), channel_id=1, source_target_pairs={{0,4},{3,31},{4,8},{7,3},{8,12},{11,7},{12,16},{15,11},{16,20},{19... | collective-permute-start | bytes 7280648 | tf_op jit(solution)/shard_map/ppermute | solution.py:928
  8.3 14.2 %collective-permute-start.1 = (bf16[2192,128]{1,0:T(8,128)(2,1)S(1)}, bf16[2192,128]{1,0:T(8,128)(2,1)S(1)}, u32[]{:S(2)}, u32[]{:S(2)}) collective-permute-start(bf16[2192,128]{1,0:T(8,128)(2,1)S(1)} %get-tuple-element.20.own_ref.refs_0_), channel_id=1, source_target_pairs={{0,2},{1,3},{2,0},{3,1},{4,6},{5,7},{6,4},{7,5},{8,10},{9,11},{10,... | collective-permute-start | bytes 1683464 | tf_op jit(solution)/shard_map/ppermute | solution.py:930
  8.4 18.1 %copy-start.12 = (bf16[4,22528]{1,0:T(4,128)(2,1)S(1)}, bf16[4,22528]{1,0:T(4,128)(2,1)}, u32[]{:S(2)}) copy-start(bf16[4,22528]{1,0:T(4,128)(2,1)} %features_ref.3) | copy-start | bytes 540676
  38.1 14.6 %copy-start.6 = (f32[512]{0:T(512)S(1)}, f32[512]{0:T(512)}, u32[]{:S(2)}) copy-start(f32[512]{0:T(512)} %param.27) | copy-start | bytes 6148
